TPU v7x, 128 devices: a whole 4x4x4 slice. The times are simulated.
128 devices in a mesh: space: 64 (over x_lo, z, y, core), peer: 2 (over x_hi).
Axes of the slice: x: 4 (x_hi: 2, x_lo: 2; x = x_hi * 2 + x_lo), y: 4, z: 4, core: 2. Of those that a mesh axis runs over, the one named last changes fastest.
Arguments:
- wavefield: float32 [2, 9, 512, 64, 128], P('peer', None, 'space'), may hold values from -100 to 100
- buoyancy: float32 [512, 64, 128], P('space'), may hold values from 0.2 to 0.5
- lame_lambda: float32 [512, 64, 128], P('space'), may hold values from 0.06 to 0.12
- shear_modulus: float32 [512, 64, 128], P('space'), may hold values from 0.05 to 0.1
- scale_exponents: int32 [9, 64, 8, 16], P(None, 'space'), may hold values from -2 to 2
- source_cells: int32 [2, 8], replicated, may hold values from 0 to 4194303
- wavelet: float32 [2, 3, 8], replicated, may hold values from -18 to 18
Outputs:
- final_field: float32 [2, 9, 512, 64, 128], P('peer', None, 'space')
- stored: bfloat16 [2, 3, 9, 512, 64, 128], P('peer', None, None, 'space')
- statistics: float32 [2, 3, 2], P('peer')
All inputs are finite; a program needn't handle non-finite values.
Results may differ from a plain program's by a relative error of at most 0.0045.
Values may be sent and summed in bfloat16 or wider, within the bound.
A program may use at most 64 MiB of HBM per device.

v0:
```python
import jax
import jax.numpy as jnp
from jax import lax
from jax.sharding import PartitionSpec as P

BLOCK = 8
STEPS = 3


stencil_reach = 2
stencil_weights = (9.0 / 8.0, -1.0 / 24.0)
clip_level = 4.0
energy_floor = 1e-06


def extended(cells, sides, width):
    for axis, dim in sides:
        count = lax.axis_size(axis)
        ends = count - 1
        head = lax.slice_in_dim(cells, 0, width, axis=dim)
        tail = lax.slice_in_dim(cells, cells.shape[dim] - width, cells.shape[dim], axis=dim)
        cells = jnp.concatenate(
            [
                lax.ppermute(tail, axis, [(i, (i + 1) % count) for i in range(ends)]),
                cells,
                lax.ppermute(head, axis, [((i + 1) % count, i) for i in range(ends)]),
            ],
            axis=dim,
        )
    return cells


def from_partner(block, axis, bit):
    count = lax.axis_size(axis)
    route = []
    for low in range(count):
        high = low | 1 << bit
        if high != low and high < count:
            route += [(low, high), (high, low)]
    return lax.ppermute(block, axis, route)


def copy_for_each(array, axis):
    count = lax.axis_size(axis)
    return lax.all_to_all(
        jnp.broadcast_to(array[None], (count, *array.shape)), axis, 0, 0, tiled=True
    )


def over_copies(array, axis):
    everything = copy_for_each(array, axis)
    return jnp.sum(everything, axis=0)


def pad_along(values, dimension):
    widths = [(0, 0)] * values.ndim
    widths[dimension] = (stencil_reach, stencil_reach)
    return jnp.pad(values, widths)


def derivative(padded, dimension, forward):
    length = padded.shape[dimension] - 2 * stencil_reach
    summed = None
    for offset in range(1, stencil_reach + 1):
        weight = stencil_weights[offset - 1]
        if forward:
            above_at = stencil_reach + offset
            below_at = stencil_reach + 1 - offset
        else:
            above_at = stencil_reach + offset - 1
            below_at = stencil_reach - offset
        portion = weight * (
            lax.slice_in_dim(padded, above_at, above_at + length, axis=dimension)
            - lax.slice_in_dim(padded, below_at, below_at + length, axis=dimension)
        )
        summed = portion if summed is None else summed + portion
    return summed


def differ(values, dimension, forward):
    return derivative(pad_along(values, dimension), dimension, forward)


def advance(current, buoyancy, lame_lambda, shear_modulus, images, stress_padder, velocity_padder):
    velocity = [current[:, component] for component in range(3)]
    stress = [current[:, component] for component in range(3, 9)]
    depth_rims = stress_padder(current[:, 6:9])
    velocity[0] = velocity[0] + buoyancy * (
        differ(stress[0], 3, True)
        + differ(stress[2], 2, False)
        + derivative(depth_rims[:, 1], 1, False)
    )
    velocity[1] = velocity[1] + buoyancy * (
        differ(stress[2], 3, False)
        + differ(stress[1], 2, True)
        + derivative(depth_rims[:, 2], 1, False)
    )
    velocity[2] = velocity[2] + buoyancy * (
        differ(stress[4], 3, False)
        + differ(stress[5], 2, False)
        + derivative(depth_rims[:, 0], 1, True)
    )
    depth_rims = velocity_padder(jnp.stack(velocity, axis=1))
    strain = [
        differ(velocity[0], 3, False),
        differ(velocity[1], 2, False),
        derivative(depth_rims[:, 2], 1, False),
    ]
    dilation = strain[0] + strain[1] + strain[2]
    pressure = lame_lambda * dilation + images
    stress[0] = stress[0] + pressure + 2.0 * shear_modulus * strain[0]
    stress[1] = stress[1] + pressure + 2.0 * shear_modulus * strain[1]
    stress[3] = stress[3] + pressure + 2.0 * shear_modulus * strain[2]
    stress[2] = stress[2] + shear_modulus * (
        differ(velocity[0], 2, True) + differ(velocity[1], 3, True)
    )
    stress[4] = stress[4] + shear_modulus * (
        derivative(depth_rims[:, 0], 1, True) + differ(velocity[2], 3, True)
    )
    stress[5] = stress[5] + shear_modulus * (
        derivative(depth_rims[:, 1], 1, True) + differ(velocity[2], 2, True)
    )
    return jnp.stack(velocity + stress, axis=1)


def scale_tables(exponents):
    expanded = jnp.repeat(
        jnp.repeat(jnp.repeat(exponents, BLOCK, axis=1), BLOCK, axis=2), BLOCK, axis=3
    )
    upscale = jnp.zeros(expanded.shape, jnp.float32)
    downscale = jnp.zeros(expanded.shape, jnp.float32)
    for exponent in range(-2, 3):
        chosen = expanded == exponent
        upscale = jnp.where(chosen, jnp.float32(2.0**exponent), upscale)
        downscale = jnp.where(chosen, jnp.float32(2.0 ** (-exponent)), downscale)
    return (upscale, downscale)


def compress(current, upscale, downscale):
    payload = jnp.clip(current * downscale, -clip_level, clip_level).astype(jnp.bfloat16)
    levels = lax.optimization_barrier(payload).astype(jnp.float32)
    return (payload, levels, levels * upscale)


def finish(sums, cell_count):
    mean_size = sums[..., 0] / cell_count
    relative = sums[..., 1] / cell_count / (sums[..., 2] / cell_count + energy_floor)
    return jnp.stack([mean_size, jnp.sqrt(relative)], axis=-1)


def per_device(
    wavefield, buoyancy, lame_lambda, shear_modulus, scale_exponents, source_cells, wavelet
):
    peer_rank = lax.axis_index("peer")
    slab_rank = lax.axis_index("space")
    depth_cells = wavefield.shape[2]
    row_count = wavefield.shape[3]
    columns = wavefield.shape[4]
    slab_size = depth_cells * row_count * columns
    cell_count = 9 * slab_size * lax.axis_size("space")
    upscale, downscale = scale_tables(scale_exponents)

    def stress_padder(stack):
        return extended(stack.astype(jnp.bfloat16), (("space", 2),), stencil_reach).astype(
            stack.dtype
        )

    def velocity_padder(stack):
        return extended(stack.astype(jnp.bfloat16), (("space", 2),), stencil_reach).astype(
            stack.dtype
        )

    def local_sources(shot_index, instant):
        local_index = source_cells[shot_index] - slab_rank * slab_size
        inside = (local_index >= 0) & (local_index < slab_size)
        placed = jnp.where(inside, local_index, slab_size)
        flat = (
            jnp.zeros((slab_size,), jnp.float32)
            .at[placed]
            .add(wavelet[shot_index, instant], mode="drop")
        )
        return flat.reshape(depth_cells, row_count, columns)

    current = wavefield
    shot_list = [peer_rank]
    stored_list = []
    local_sums = []
    for instant in range(STEPS):
        images = jnp.stack([local_sources(shot_index, instant) for shot_index in shot_list], axis=0)
        current = advance(
            current, buoyancy, lame_lambda, shear_modulus, images, stress_padder, velocity_padder
        )
        payload, levels, restored = compress(current, upscale, downscale)
        stored_list.append(from_partner(payload, "peer", 0)[0])
        misfit = current[0] - restored[0]
        step_terms = jnp.stack(
            [
                jnp.sum(jnp.abs(levels[0])),
                jnp.sum(misfit * misfit),
                jnp.sum(current[0] * current[0]),
            ]
        )
        local_sums.append(step_terms)
    totals = over_copies(jnp.stack(local_sums, axis=0), "space")
    statistics = finish(totals, cell_count)[None]
    stored = jnp.stack(stored_list, axis=0)[None]
    return (current, stored, statistics)


def solution(mesh):
    return jax.shard_map(
        per_device,
        mesh=mesh,
        in_specs=(
            P("peer", None, "space", None, None),
            P("space", None, None),
            P("space", None, None),
            P("space", None, None),
            P(None, "space", None, None),
            P(),
            P(),
        ),
        out_specs=(
            P("peer", None, "space", None, None),
            P("peer", None, None, "space", None, None),
            P("peer", None, None),
        ),
        check_vma=False,
    )
```

profile of v0, /device:TPU:2, one launch (start us, length us, event | category | flops | bytes accessed | tf_op | source)
XLA Modules:
  0.0 193.2 jit_solution(3914774281843952645)
XLA Ops:
  0.6 2.0 %convert.93 = bf16[1,9,8,64,128]{4,3,2,1,0:T(8,128)(2,1)S(1)} convert(f32[1,9,8,64,128]{4,3,2,1,0:T(8,128)} %param.7) | non-fusion elementwise | flops 589824 | bytes 3538944 | tf_op jit(solution)/shard_map/convert.30
  2.7 0.7 fusion.373
  3.4 1.9 collective-permute-start
  5.3 7.9 %collective-permute-start.1 = (bf16[1,3,2,64,128]{4,3,2,1,0:T(8,128)(2,1)}, bf16[1,3,2,64,128]{4,3,2,1,0:T(8,128)(2,1)}, u32[]{:S(2)}, u32[]{:S(2)}) collective-permute-start(bf16[1,3,2,64,128]{4,3,2,1,0:T(8,128)(2,1)} %get-tuple-element.96), channel_id=1, source_target_pairs={{2,0},{4,2},{6,4},{8,6},{10,8},{12,10},{14,12},{16,14},{18,16},{20... | collective-permute-start | bytes 294920 | tf_op jit(solution)/shard_map/ppermute | solution.py:26
  13.2 0.8 slice.936
  14.0 1.0 slice_bitcast_fusion.19
  15.5 0.7 broadcast_bitcast_fusion.4
  16.5 0.7 broadcast_bitcast_fusion.3
  17.4 0.7 broadcast_bitcast_fusion.2
  18.3 0.7 broadcast_bitcast_fusion.6
  19.1 1.1 copy.57
  20.1 0.9 broadcast_bitcast_fusion
  21.1 1.3 scatter_custom_fusion
  22.4 1.3 scatter_custom_fusion.1
  23.7 1.3 scatter_custom_fusion.2
  25.2 1.8 copy.50
  27.0 1.8 copy.52
  28.8 1.7 copy.54
  30.5 0.9 copy.56
  31.4 1.3 copy.58
  32.8 1.2 maximum_convert_fusion
  34.1 0.3 bitcast_dynamic-update-slice_fusion.23
  34.4 0.5 copy-done.9
  34.9 0.3 bitcast_dynamic-update-slice_fusion.22
  35.2 0.3 bitcast_dynamic-update-slice_fusion.21
  35.6 0.3 fusion.383
  35.9 1.9 collective-permute-start.2
  37.9 7.9 %collective-permute-start.3 = (bf16[1,3,2,64,128]{4,3,2,1,0:T(8,128)(2,1)S(1)}, bf16[1,3,2,64,128]{4,3,2,1,0:T(8,128)(2,1)S(1)}, u32[]{:S(2)}, u32[]{:S(2)}) collective-permute-start(bf16[1,3,2,64,128]{4,3,2,1,0:T(8,128)(2,1)S(1)} %get-tuple-element.111), channel_id=1, source_target_pairs={{2,0},{4,2},{6,4},{8,6},{10,8},{12,10},{14,12},{16,14},{18,16},{20... | collective-permute-start | bytes 294920 | tf_op jit(solution)/shard_map/ppermute | solution.py:26
  46.1 1.8 collective-permute-done.3
  48.5 0.3 bitcast_dynamic-update-slice_fusion.3
  48.9 0.3 bitcast_dynamic-update-slice_fusion.19
  49.5 1.9 collective-permute-start.4
  51.5 8.0 %collective-permute-start.5 = (bf16[1,3,2,64,128]{4,3,2,1,0:T(8,128)(2,1)S(1)}, bf16[1,3,2,64,128]{4,3,2,1,0:T(8,128)(2,1)S(1)}, u32[]{:S(2)}, u32[]{:S(2)}) collective-permute-start(bf16[1,3,2,64,128]{4,3,2,1,0:T(8,128)(2,1)S(1)} %get-tuple-element.109), channel_id=1, source_target_pairs={{2,0},{4,2},{6,4},{8,6},{10,8},{12,10},{14,12},{16,14},{18,16},{20... | collective-permute-start | bytes 294920 | tf_op jit(solution)/shard_map/ppermute | solution.py:26
  59.5 0.3 collective-permute-done.4
  59.8 1.8 collective-permute-done.5
  61.8 0.3 bitcast_dynamic-update-slice_fusion.17
  62.1 0.3 bitcast_dynamic-update-slice_fusion.16
  62.4 0.3 bitcast_dynamic-update-slice_fusion.15
  63.1 1.9 collective-permute-start.6
  65.0 8.0 %collective-permute-start.7 = (bf16[1,3,2,64,128]{4,3,2,1,0:T(8,128)(2,1)S(1)}, bf16[1,3,2,64,128]{4,3,2,1,0:T(8,128)(2,1)S(1)}, u32[]{:S(2)}, u32[]{:S(2)}) collective-permute-start(bf16[1,3,2,64,128]{4,3,2,1,0:T(8,128)(2,1)S(1)} %get-tuple-element.107), channel_id=1, source_target_pairs={{2,0},{4,2},{6,4},{8,6},{10,8},{12,10},{14,12},{16,14},{18,16},{20... | collective-permute-start | bytes 294920 | tf_op jit(solution)/shard_map/ppermute | solution.py:26
  73.1 0.3 collective-permute-done.6
  73.4 1.8 collective-permute-done.7
  75.8 0.3 bitcast_dynamic-update-slice_fusion
  76.8 1.9 collective-permute-start.8
  78.7 8.0 %collective-permute-start.9 = (bf16[1,3,2,64,128]{4,3,2,1,0:T(8,128)(2,1)S(1)}, bf16[1,3,2,64,128]{4,3,2,1,0:T(8,128)(2,1)S(1)}, u32[]{:S(2)}, u32[]{:S(2)}) collective-permute-start(bf16[1,3,2,64,128]{4,3,2,1,0:T(8,128)(2,1)S(1)} %get-tuple-element.105), channel_id=1, source_target_pairs={{2,0},{4,2},{6,4},{8,6},{10,8},{12,10},{14,12},{16,14},{18,16},{20... | collective-permute-start | bytes 294920 | tf_op jit(solution)/shard_map/ppermute | solution.py:26
  86.7 0.3 collective-permute-done.8
  87.0 1.8 collective-permute-done.9
  89.1 0.5 fusion.369
  89.9 0.3 fusion.371
  90.3 1.9 collective-permute-start.10
  92.2 8.1 %collective-permute-start.11 = (bf16[1,3,2,64,128]{4,3,2,1,0:T(8,128)(2,1)S(1)}, bf16[1,3,2,64,128]{4,3,2,1,0:T(8,128)(2,1)S(1)}, u32[]{:S(2)}, u32[]{:S(2)}) collective-permute-start(bf16[1,3,2,64,128]{4,3,2,1,0:T(8,128)(2,1)S(1)} %get-tuple-element.103), channel_id=1, source_target_pairs={{2,0},{4,2},{6,4},{8,6},{10,8},{12,10},{14,12},{16,14},{18,16},{20... | collective-permute-start | bytes 294920 | tf_op jit(solution)/shard_map/ppermute | solution.py:26
  100.6 1.8 collective-permute-done.11
  103.7 0.5 copy-done.5
  104.3 2.6 %clamp_convert_fusion.2 = (bf16[1,9,8,64,128]{4,3,2,1,0:T(8,128)(2,1)}, bf16[1,9,8,64,128]{4,3,2,1,0:T(8,128)(2,1)}, bf16[1,9,8,64,128]{4,3,2,1,0:T(8,128)(2,1)}) fusion(f32[1,9,8,64,128]{4,3,2,1,0:T(8,128)S(1)} %get-tuple-element.20, f32[9,64,128]{2,1,0:T(8,128)S(1)} %copy-done.5, pred[9,64,128]{2,1,0:T(8,128)(4,1)S(1)} %copy-done.15, ...), kind=kLoop, calls=%fused_computation.28 | loop fusion | flops 7667712 | bytes 11206656 | tf_op jit(solution)/shard_map/convert_element_type | solution.py:140
  106.9 3.0 %collective-permute-start.12 = (bf16[1,9,8,64,128]{4,3,2,1,0:T(8,128)(2,1)}, bf16[1,9,8,64,128]{4,3,2,1,0:T(8,128)(2,1)}, u32[]{:S(2)}, u32[]{:S(2)}) collective-permute-start(bf16[1,9,8,64,128]{4,3,2,1,0:T(8,128)(2,1)} %get-tuple-element.97), channel_id=1, source_target_pairs={{0,1},{1,0},{2,3},{3,2},{4,5},{5,4},{6,7},{7,6},{8,9},{9,8},{10,11... | collective-permute-start | bytes 3538952 | tf_op jit(solution)/shard_map/ppermute | solution.py:40
  109.9 0.5 collective-permute-start.13
  110.4 3.0 %collective-permute-start.14 = (bf16[1,9,8,64,128]{4,3,2,1,0:T(8,128)(2,1)}, bf16[1,9,8,64,128]{4,3,2,1,0:T(8,128)(2,1)}, u32[]{:S(2)}, u32[]{:S(2)}) collective-permute-start(bf16[1,9,8,64,128]{4,3,2,1,0:T(8,128)(2,1)} %get-tuple-element.98), channel_id=1, source_target_pairs={{0,1},{1,0},{2,3},{3,2},{4,5},{5,4},{6,7},{7,6},{8,9},{9,8},{10,11... | collective-permute-start | bytes 3538952 | tf_op jit(solution)/shard_map/ppermute | solution.py:40
  113.4 4.5 %fusion.11 = (f32[]{:T(128)}, f32[]{:T(128)}, f32[]{:T(128)}, f32[]{:T(128)}, f32[]{:T(128)}, /*index=5*/f32[]{:T(128)}, f32[]{:T(128)}, f32[]{:T(128)}, f32[]{:T(128)}) fusion(f32[1,9,8,64,128]{4,3,2,1,0:T(8,128)S(1)} %fusion.157, bf16[1,9,8,64,128]{4,3,2,1,0:T(8,128)(2,1)} %get-tuple-element.98, f32[9,64,128]{2,1,0:T(8,128)S(1)} %copy.58, ...), kind=kLoop, calls=%fused_computation.21 | loop fusion | flops 18284536 | bytes 11206692 | tf_op jit(solution)/shard_map/reduce_sum | solution.py:199
  117.9 1.9 %maximum_bitcast_fusion.6 = f32[1,3]{1,0:T(1,128)S(1)} fusion(f32[1]{0:T(128)} %bitcast.92, f32[1]{0:T(128)} %bitcast.91, f32[1]{0:T(128)} %bitcast.87), kind=kLoop, calls=%fused_computation.632 | loop fusion | flops 6 | bytes 24 | tf_op jit(solution)/shard_map/stack | solution.py:204
  119.8 1.9 %maximum_bitcast_fusion.7 = f32[1,3]{1,0:T(1,128)S(1)} fusion(f32[1]{0:T(128)} %bitcast.96, f32[1]{0:T(128)} %bitcast.95, f32[1]{0:T(128)} %bitcast.94), kind=kLoop, calls=%fused_computation.633 | loop fusion | flops 6 | bytes 24 | tf_op jit(solution)/shard_map/stack | solution.py:204
  121.7 2.0 %maximum_bitcast_fusion.8 = f32[1,3]{1,0:T(1,128)S(1)} fusion(f32[1]{0:T(128)} %bitcast.100, f32[1]{0:T(128)} %bitcast.99, f32[1]{0:T(128)} %bitcast.98), kind=kLoop, calls=%fused_computation.634 | loop fusion | flops 6 | bytes 24 | tf_op jit(solution)/shard_map/stack | solution.py:204
  123.8 65.0 %all_to_all.5 = f32[64,3,3]{2,1,0:T(4,128)S(1)} all-to-all(f32[64,3,3]{2,1,0:T(4,128)S(1)} %broadcast_in_dim.157), channel_id=1, replica_groups=mesh['space'=64,'peer'=2] {'space'}, dimensions={0} | all-to-all | bytes 4608 | tf_op jit(solution)/shard_map/all_to_all | solution.py:45
  189.1 0.7 copy.60
  189.8 3.4 %maximum_bitcast_fusion = bf16[1,3,9,8,64,128]{5,4,3,2,1,0:T(8,128)(2,1)} fusion(bf16[1,9,8,64,128]{4,3,2,1,0:T(8,128)(2,1)} %collective-permute-done.14, bf16[1,9,8,64,128]{4,3,2,1,0:T(8,128)(2,1)} %collective-permute-done.13, bf16[1,9,8,64,128]{4,3,2,1,0:T(8,128)(2,1)} %collective-permute-done.12), kind=kLoop, calls=%fused_computation.3 | loop fusion | flops 3538944 | bytes 7077888 | tf_op jit(solution)/shard_map/broadcast_in_dim | solution.py:206
  (116 shorter events, 7.1 us)
Async XLA Ops:
  0.6 13.3 %copy-start.2 = (f32[1,9,8,64,128]{4,3,2,1,0:T(8,128)S(1)}, f32[1,9,8,64,128]{4,3,2,1,0:T(8,128)}, u32[]{:S(2)}) copy-start(f32[1,9,8,64,128]{4,3,2,1,0:T(8,128)} %param.7) | copy-start | bytes 7077892
  2.7 12.3 %copy-start.16 = (s32[9,1,8,16]{3,2,1,0:T(8,128)S(1)}, s32[9,1,8,16]{3,2,1,0:T(8,128)}, u32[]{:S(2)}) copy-start(s32[9,1,8,16]{3,2,1,0:T(8,128)} %param.11) | copy-start | bytes 13828
  3.4 29.4 %collective-permute-start = (bf16[1,3,2,64,128]{4,3,2,1,0:T(8,128)(2,1)}, bf16[1,3,2,64,128]{4,3,2,1,0:T(8,128)(2,1)}, u32[]{:S(2)}, u32[]{:S(2)}) collective-permute-start(bf16[1,3,2,64,128]{4,3,2,1,0:T(8,128)(2,1)} %get-tuple-element.95), channel_id=1, source_target_pairs={{0,2},{2,4},{4,6},{6,8},{8,10},{10,12},{12,14},{14,16},{16,18},{18... | collective-permute-start | bytes 294920 | tf_op jit(solution)/shard_map/ppermute | solution.py:24
  5.3 27.5 %collective-permute-start.1 = (bf16[1,3,2,64,128]{4,3,2,1,0:T(8,128)(2,1)}, bf16[1,3,2,64,128]{4,3,2,1,0:T(8,128)(2,1)}, u32[]{:S(2)}, u32[]{:S(2)}) collective-permute-start(bf16[1,3,2,64,128]{4,3,2,1,0:T(8,128)(2,1)} %get-tuple-element.96), channel_id=1, source_target_pairs={{2,0},{4,2},{6,4},{8,6},{10,8},{12,10},{14,12},{16,14},{18,16},{20... | collective-permute-start | bytes 294920 | tf_op jit(solution)/shard_map/ppermute | solution.py:26
  15.0 6.0 %copy-start.17 = (f32[2,3,8]{2,0,1:T(2,128)S(1)}, f32[2,3,8]{2,0,1:T(2,128)}, u32[]{:S(2)}) copy-start(f32[2,3,8]{2,0,1:T(2,128)} %param.13) | copy-start | bytes 580
  15.0 6.0 %copy-start.18 = (s32[2,8]{1,0:T(2,128)S(1)}, s32[2,8]{1,0:T(2,128)}, u32[]{:S(2)}) copy-start(s32[2,8]{1,0:T(2,128)} %param.12) | copy-start | bytes 196
  31.4 2.6 %copy-start.1 = (f32[8,64,128]{2,1,0:T(8,128)S(1)}, f32[8,64,128]{2,1,0:T(8,128)}, u32[]{:S(2)}) copy-start(f32[8,64,128]{2,1,0:T(8,128)} %param.8) | copy-start | bytes 786436
  31.4 2.6 %copy-start.10 = (f32[1,8,64,128]{3,2,1,0:T(8,128)S(1)}, f32[1,8,64,128]{3,2,1,0:T(8,128)}, u32[]{:S(2)}) copy-start(f32[1,8,64,128]{3,2,1,0:T(8,128)} %get-tuple-element.75) | copy-start | bytes 786436
  33.9 1.0 copy-start.9
  34.1 1.1 copy-start.7
  34.1 1.1 copy-start.8
  35.9 10.2 %collective-permute-start.2 = (bf16[1,3,2,64,128]{4,3,2,1,0:T(8,128)(2,1)S(1)}, bf16[1,3,2,64,128]{4,3,2,1,0:T(8,128)(2,1)S(1)}, u32[]{:S(2)}, u32[]{:S(2)}) collective-permute-start(bf16[1,3,2,64,128]{4,3,2,1,0:T(8,128)(2,1)S(1)} %get-tuple-element.110), channel_id=1, source_target_pairs={{0,2},{2,4},{4,6},{6,8},{8,10},{10,12},{12,14},{14,16},{16,18},{18... | collective-permute-start | bytes 294920 | tf_op jit(solution)/shard_map/ppermute | solution.py:24
  37.9 10.1 %collective-permute-start.3 = (bf16[1,3,2,64,128]{4,3,2,1,0:T(8,128)(2,1)S(1)}, bf16[1,3,2,64,128]{4,3,2,1,0:T(8,128)(2,1)S(1)}, u32[]{:S(2)}, u32[]{:S(2)}) collective-permute-start(bf16[1,3,2,64,128]{4,3,2,1,0:T(8,128)(2,1)S(1)} %get-tuple-element.111), channel_id=1, source_target_pairs={{2,0},{4,2},{6,4},{8,6},{10,8},{12,10},{14,12},{16,14},{18,16},{20... | collective-permute-start | bytes 294920 | tf_op jit(solution)/shard_map/ppermute | solution.py:26
  45.7 2.4 %copy-start = (f32[8,64,128]{2,1,0:T(8,128)S(1)}, f32[8,64,128]{2,1,0:T(8,128)}, u32[]{:S(2)}) copy-start(f32[8,64,128]{2,1,0:T(8,128)} %param.10) | copy-start | bytes 786436
  45.7 2.4 %copy-start.4 = (f32[8,64,128]{2,1,0:T(8,128)S(1)}, f32[8,64,128]{2,1,0:T(8,128)}, u32[]{:S(2)}) copy-start(f32[8,64,128]{2,1,0:T(8,128)} %param.9) | copy-start | bytes 786436
  45.8 2.4 %copy-start.12 = (f32[65536]{0:T(1024)S(1)}, f32[65536]{0:T(1024)}, u32[]{:S(2)}) copy-start(f32[65536]{0:T(1024)} %scatter_custom_fusion) | copy-start | bytes 786436
  49.5 10.2 %collective-permute-start.4 = (bf16[1,3,2,64,128]{4,3,2,1,0:T(8,128)(2,1)S(1)}, bf16[1,3,2,64,128]{4,3,2,1,0:T(8,128)(2,1)S(1)}, u32[]{:S(2)}, u32[]{:S(2)}) collective-permute-start(bf16[1,3,2,64,128]{4,3,2,1,0:T(8,128)(2,1)S(1)} %get-tuple-element.108), channel_id=1, source_target_pairs={{0,2},{2,4},{4,6},{6,8},{8,10},{10,12},{12,14},{14,16},{16,18},{18... | collective-permute-start | bytes 294920 | tf_op jit(solution)/shard_map/ppermute | solution.py:24
  51.5 10.2 %collective-permute-start.5 = (bf16[1,3,2,64,128]{4,3,2,1,0:T(8,128)(2,1)S(1)}, bf16[1,3,2,64,128]{4,3,2,1,0:T(8,128)(2,1)S(1)}, u32[]{:S(2)}, u32[]{:S(2)}) collective-permute-start(bf16[1,3,2,64,128]{4,3,2,1,0:T(8,128)(2,1)S(1)} %get-tuple-element.109), channel_id=1, source_target_pairs={{2,0},{4,2},{6,4},{8,6},{10,8},{12,10},{14,12},{16,14},{18,16},{20... | collective-permute-start | bytes 294920 | tf_op jit(solution)/shard_map/ppermute | solution.py:26
  63.1 10.2 %collective-permute-start.6 = (bf16[1,3,2,64,128]{4,3,2,1,0:T(8,128)(2,1)S(1)}, bf16[1,3,2,64,128]{4,3,2,1,0:T(8,128)(2,1)S(1)}, u32[]{:S(2)}, u32[]{:S(2)}) collective-permute-start(bf16[1,3,2,64,128]{4,3,2,1,0:T(8,128)(2,1)S(1)} %get-tuple-element.106), channel_id=1, source_target_pairs={{0,2},{2,4},{4,6},{6,8},{8,10},{10,12},{12,14},{14,16},{16,18},{18... | collective-permute-start | bytes 294920 | tf_op jit(solution)/shard_map/ppermute | solution.py:24
  65.0 10.2 %collective-permute-start.7 = (bf16[1,3,2,64,128]{4,3,2,1,0:T(8,128)(2,1)S(1)}, bf16[1,3,2,64,128]{4,3,2,1,0:T(8,128)(2,1)S(1)}, u32[]{:S(2)}, u32[]{:S(2)}) collective-permute-start(bf16[1,3,2,64,128]{4,3,2,1,0:T(8,128)(2,1)S(1)} %get-tuple-element.107), channel_id=1, source_target_pairs={{2,0},{4,2},{6,4},{8,6},{10,8},{12,10},{14,12},{16,14},{18,16},{20... | collective-permute-start | bytes 294920 | tf_op jit(solution)/shard_map/ppermute | solution.py:26
  73.0 2.4 %copy-start.11 = (f32[65536]{0:T(1024)S(1)}, f32[65536]{0:T(1024)}, u32[]{:S(2)}) copy-start(f32[65536]{0:T(1024)} %scatter_custom_fusion.1) | copy-start | bytes 786436
  76.8 10.2 %collective-permute-start.8 = (bf16[1,3,2,64,128]{4,3,2,1,0:T(8,128)(2,1)S(1)}, bf16[1,3,2,64,128]{4,3,2,1,0:T(8,128)(2,1)S(1)}, u32[]{:S(2)}, u32[]{:S(2)}) collective-permute-start(bf16[1,3,2,64,128]{4,3,2,1,0:T(8,128)(2,1)S(1)} %get-tuple-element.104), channel_id=1, source_target_pairs={{0,2},{2,4},{4,6},{6,8},{8,10},{10,12},{12,14},{14,16},{16,18},{18... | collective-permute-start | bytes 294920 | tf_op jit(solution)/shard_map/ppermute | solution.py:24
  78.7 10.2 %collective-permute-start.9 = (bf16[1,3,2,64,128]{4,3,2,1,0:T(8,128)(2,1)S(1)}, bf16[1,3,2,64,128]{4,3,2,1,0:T(8,128)(2,1)S(1)}, u32[]{:S(2)}, u32[]{:S(2)}) collective-permute-start(bf16[1,3,2,64,128]{4,3,2,1,0:T(8,128)(2,1)S(1)} %get-tuple-element.105), channel_id=1, source_target_pairs={{2,0},{4,2},{6,4},{8,6},{10,8},{12,10},{14,12},{16,14},{18,16},{20... | collective-permute-start | bytes 294920 | tf_op jit(solution)/shard_map/ppermute | solution.py:26
  90.3 10.2 %collective-permute-start.10 = (bf16[1,3,2,64,128]{4,3,2,1,0:T(8,128)(2,1)S(1)}, bf16[1,3,2,64,128]{4,3,2,1,0:T(8,128)(2,1)S(1)}, u32[]{:S(2)}, u32[]{:S(2)}) collective-permute-start(bf16[1,3,2,64,128]{4,3,2,1,0:T(8,128)(2,1)S(1)} %get-tuple-element.102), channel_id=1, source_target_pairs={{0,2},{2,4},{4,6},{6,8},{8,10},{10,12},{12,14},{14,16},{16,18},{18... | collective-permute-start | bytes 294920 | tf_op jit(solution)/shard_map/ppermute | solution.py:24
  92.2 10.2 %collective-permute-start.11 = (bf16[1,3,2,64,128]{4,3,2,1,0:T(8,128)(2,1)S(1)}, bf16[1,3,2,64,128]{4,3,2,1,0:T(8,128)(2,1)S(1)}, u32[]{:S(2)}, u32[]{:S(2)}) collective-permute-start(bf16[1,3,2,64,128]{4,3,2,1,0:T(8,128)(2,1)S(1)} %get-tuple-element.103), channel_id=1, source_target_pairs={{2,0},{4,2},{6,4},{8,6},{10,8},{12,10},{14,12},{16,14},{18,16},{20... | collective-permute-start | bytes 294920 | tf_op jit(solution)/shard_map/ppermute | solution.py:26
  100.4 2.1 %copy-start.6 = (f32[65536]{0:T(1024)S(1)}, f32[65536]{0:T(1024)}, u32[]{:S(2)}) copy-start(f32[65536]{0:T(1024)} %scatter_custom_fusion.2) | copy-start | bytes 786436
  103.2 1.0 copy-start.5
  103.3 1.0 copy-start.13
  103.3 1.0 copy-start.14
  103.3 1.0 copy-start.15
  103.7 9.7 %copy-start.3 = (f32[1,9,8,64,128]{4,3,2,1,0:T(8,128)}, f32[1,9,8,64,128]{4,3,2,1,0:T(8,128)S(1)}, u32[]{:S(2)}) copy-start(f32[1,9,8,64,128]{4,3,2,1,0:T(8,128)S(1)} %fusion.157) | copy-start | bytes 7077892
  106.9 82.9 %collective-permute-start.12 = (bf16[1,9,8,64,128]{4,3,2,1,0:T(8,128)(2,1)}, bf16[1,9,8,64,128]{4,3,2,1,0:T(8,128)(2,1)}, u32[]{:S(2)}, u32[]{:S(2)}) collective-permute-start(bf16[1,9,8,64,128]{4,3,2,1,0:T(8,128)(2,1)} %get-tuple-element.97), channel_id=1, source_target_pairs={{0,1},{1,0},{2,3},{3,2},{4,5},{5,4},{6,7},{7,6},{8,9},{9,8},{10,11... | collective-permute-start | bytes 3538952 | tf_op jit(solution)/shard_map/ppermute | solution.py:40
  109.9 79.9 %collective-permute-start.13 = (bf16[1,9,8,64,128]{4,3,2,1,0:T(8,128)(2,1)}, bf16[1,9,8,64,128]{4,3,2,1,0:T(8,128)(2,1)}, u32[]{:S(2)}, u32[]{:S(2)}) collective-permute-start(bf16[1,9,8,64,128]{4,3,2,1,0:T(8,128)(2,1)} %get-tuple-element.99), channel_id=1, source_target_pairs={{0,1},{1,0},{2,3},{3,2},{4,5},{5,4},{6,7},{7,6},{8,9},{9,8},{10,11... | collective-permute-start | bytes 3538952 | tf_op jit(solution)/shard_map/ppermute | solution.py:40
  110.4 79.4 %collective-permute-start.14 = (bf16[1,9,8,64,128]{4,3,2,1,0:T(8,128)(2,1)}, bf16[1,9,8,64,128]{4,3,2,1,0:T(8,128)(2,1)}, u32[]{:S(2)}, u32[]{:S(2)}) collective-permute-start(bf16[1,9,8,64,128]{4,3,2,1,0:T(8,128)(2,1)} %get-tuple-element.98), channel_id=1, source_target_pairs={{0,1},{1,0},{2,3},{3,2},{4,5},{5,4},{6,7},{7,6},{8,9},{9,8},{10,11... | collective-permute-start | bytes 3538952 | tf_op jit(solution)/shard_map/ppermute | solution.py:40
where the time goes:
time: 194 us; the launch traced here: 193 us
  starting transfers between devices  65.8 us (34%)
  blocking collectives  65 us (34%)
  other arithmetic  31.9 us (16%)
  local copies, waits for them, and re-layouts  18.6 us (10%)
  waiting for transfers between devices  10.4 us (5%)
    all_to_all x1, blocking collectives, copy_for_each(): lax.all_to_all(jnp.broadcast_to(array[None], (count, *array.shape)), axis...  65 us
    ppermute x6, starting transfers between devices, extended(): lax.ppermute(head, axis, [((i + 1) % count, i) for i in range(ends)])  47.7 us
    ppermute x6, starting transfers between devices, extended(): lax.ppermute(tail, axis, [(i, (i + 1) % count) for i in range(ends)])  11.5 us
    ppermute x6, waiting for transfers between devices, extended(): lax.ppermute(head, axis, [((i + 1) % count, i) for i in range(ends)])  9.17 us
    eq x14, local copies, waits for them, and re-layouts, scale_tables(): chosen = expanded == exponent  8.55 us
    ppermute x3, starting transfers between devices, from_partner(): return lax.ppermute(block, axis, route)  6.53 us
    another operation x4, other arithmetic, per_device(): totals = over_copies(jnp.stack(local_sums, axis=0), 'space')  5.94 us
    unnamed x21, other arithmetic  4.65 us
  transfers between devices with their start and end apart: 15, of which 10 were waited for; matrix products, arithmetic and copies ran while one was open for 16% of the time, Pallas kernels for 0%

commit v1 on v0

v1 whole, which is shorter than its diff:
```python
import functools

import jax
import jax.numpy as jnp
from jax import lax
from jax.experimental import pallas as pl
from jax.experimental.pallas import tpu as pltpu
from jax.sharding import PartitionSpec as P

MESH = pl.DeviceIdType.MESH
F32 = jnp.float32
BF16 = jnp.bfloat16

BLOCK = 8
STEPS = 3
SOURCES = 8
DEPTH, ROWS, COLS = 8, 64, 128
PAD = 8
YB = 16
OWN = 3
FAR = 6
BUO, MOD = 5, 3
LOW = 8
ROW_CUTS = (0, 32, 48, 64)
VX, VY, VZ, SXX, SYY, SXY, SZZ, SXZ, SYZ = range(9)
clip_level = 4.0
energy_floor = 1e-06


def lanes(shape):
    return lax.broadcasted_iota(jnp.int32, shape, 1)


class Slab:
    def __init__(self, ref, lead, buoyancy, lame, shear):
        self.ref, self.lead = ref, lead
        self.buoyancy, self.lame, self.shear = buoyancy, lame, shear
        self.lane = lanes((YB, COLS))

    def at(self, part, z, y, shift=0):
        if shift == 0:
            return self.ref[part, z + self.lead, pl.ds(y + PAD, YB), :]
        window = self.ref[part, z + self.lead, pl.ds(y, YB + 2 * PAD), :]
        return window[PAD + shift : PAD + shift + YB]

    def put(self, part, z, y, value, rows):
        lo, hi = rows
        if lo > y or hi < y + YB:
            row = lax.broadcasted_iota(jnp.int32, (YB, COLS), 0) + y
            value = jnp.where((row >= lo) & (row < hi), value, self.at(part, z, y))
        self.ref[part, z + self.lead, pl.ds(y + PAD, YB), :] = value

    def along_x(self, f, forward):
        after = jnp.where(self.lane < COLS - 1, pltpu.roll(f, COLS - 1, 1), 0.0)
        before = jnp.where(self.lane >= 1, pltpu.roll(f, 1, 1), 0.0)
        if forward:
            far = jnp.where(self.lane < COLS - 2, pltpu.roll(f, COLS - 2, 1), 0.0)
            return after - f, far - before
        far = jnp.where(self.lane >= 2, pltpu.roll(f, 2, 1), 0.0)
        return f - before, after - far

    def dx(self, part, z, y, forward):
        return self.along_x(self.at(part, z, y), forward)

    def dy(self, part, z, y, forward):
        window = self.ref[part, z + self.lead, pl.ds(y, YB + 2 * PAD), :]
        get = lambda shift: window[PAD + shift : PAD + shift + YB]
        if forward:
            return get(1) - get(0), get(2) - get(-1)
        return get(0) - get(-1), get(1) - get(-2)

    def dz(self, part, z, y, forward):
        get = lambda shift: self.at(part, z + shift, y)
        if forward:
            return get(1) - get(0), get(2) - get(-1)
        return get(0) - get(-1), get(1) - get(-2)

    def mat(self, table, lead, z, y, factor):
        return table[z + lead, pl.ds(y, YB), :] * factor

    def velocity(self, part, z, y, rows):
        if part == VX:
            terms = (self.dx(SXX, z, y, True), self.dy(SXY, z, y, False), self.dz(SXZ, z, y, False))
        elif part == VY:
            terms = (self.dx(SXY, z, y, False), self.dy(SYY, z, y, True), self.dz(SYZ, z, y, False))
        else:
            terms = (self.dx(SXZ, z, y, False), self.dy(SYZ, z, y, False), self.dz(SZZ, z, y, True))
        near = terms[0][0] + terms[1][0] + terms[2][0]
        far = terms[0][1] + terms[1][1] + terms[2][1]
        change = self.mat(self.buoyancy, BUO, z, y, 1.0 / 24.0) * (27.0 * near - far)
        self.put(part, z, y, self.at(part, z, y) + change, rows)

    def shears(self, part, z, y, rows):
        if part == SXY:
            terms = (self.dy(VX, z, y, True), self.dx(VY, z, y, True))
        elif part == SXZ:
            terms = (self.dz(VX, z, y, True), self.dx(VZ, z, y, True))
        else:
            terms = (self.dz(VY, z, y, True), self.dy(VZ, z, y, True))
        near = terms[0][0] + terms[1][0]
        far = terms[0][1] + terms[1][1]
        change = self.mat(self.shear, MOD, z, y, 1.0 / 24.0) * (27.0 * near - far)
        self.put(part, z, y, self.at(part, z, y) + change, rows)

    def normals(self, z, y, rows, image):
        strain = []
        for near, far in (
            self.dx(VX, z, y, False),
            self.dy(VY, z, y, False),
            self.dz(VZ, z, y, False),
        ):
            strain.append(27.0 * near - far)
        pressure = (
            self.mat(self.lame, MOD, z, y, 1.0 / 24.0) * (strain[0] + strain[1] + strain[2])
            + image(z, y)
        )
        double = self.mat(self.shear, MOD, z, y, 2.0 / 24.0)
        for part, value in zip((SXX, SYY, SZZ), strain):
            self.put(part, z, y, self.at(part, z, y) + (pressure + double * value), rows)


def layers(count, place, rows, body):
    first = rows[0] // YB * YB

    @pl.loop(0, count)
    def _(i):
        z = place(i)
        for y in range(first, rows[1], YB):
            body(z, y)


def run_velocity(slab, count, place, deep_place, rows):
    for part in (VX, VY):
        layers(count, place, rows, lambda z, y, part=part: slab.velocity(part, z, y, rows))
    layers(count, deep_place, rows, lambda z, y: slab.velocity(VZ, z, y, rows))


def run_stress(slab, deep, plain, rows, image):
    layers(*deep, rows, lambda z, y: slab.normals(z, y, rows, image))
    layers(*plain, rows, lambda z, y: slab.shears(SXY, z, y, rows))
    layers(*deep, rows, lambda z, y: slab.shears(SXZ, z, y, rows))
    layers(*deep, rows, lambda z, y: slab.shears(SYZ, z, y, rows))


def kernel(
    slabs,
    wave_hbm, buo_hbm, lame_hbm, shear_hbm, exps, cells, wavelet,
    final_hbm, stored_hbm, stats_out,
    own, other, mirror, low_a, low_b, high_a, high_b, buo, lame, shear, got, packed,
    up_rows, down_rows, exp_rows, sums, stat_src, stat_rx,
    in_sem, out_sem, halo_send, halo_recv, mat_send, mat_recv,
    x_send, x_recv, fwd_send, fwd_recv, stat_send, stat_recv,
):
    me, peer = lax.axis_index("space"), lax.axis_index("peer")
    has_down, has_up = me > 0, me < slabs - 1
    up, down = (me + 1, peer), (me - 1, peer)
    partner = (me, 1 - peer)
    groups = slabs // LOW
    block, lane_of = me // LOW, lax.rem(me, LOW)
    near_peers = [(block * LOW + lax.rem(lane_of + k, LOW), peer) for k in range(1, LOW)]
    wide_peers = [(lax.rem(block + k, groups) * LOW + lane_of, peer) for k in range(1, groups)]

    barrier = pltpu.get_barrier_semaphore()
    for device in [partner] + near_peers + wide_peers:
        pl.semaphore_signal(barrier, inc=1, device_id=device, device_id_type=MESH)

    @pl.when(has_up)
    def _():
        pl.semaphore_signal(barrier, inc=1, device_id=up, device_id_type=MESH)

    @pl.when(has_down)
    def _():
        pl.semaphore_signal(barrier, inc=1, device_id=down, device_id_type=MESH)

    def remote(source, target, send, recv, device):
        return pltpu.make_async_remote_copy(
            src_ref=source, dst_ref=target, send_sem=send, recv_sem=recv,
            device_id=device, device_id_type=MESH,
        )

    inner = pl.ds(PAD, ROWS)
    loads = [
        pltpu.make_async_copy(
            wave_hbm.at[0, part], own.at[part, pl.ds(OWN, DEPTH), inner, :], in_sem.at[part]
        )
        for part in range(9)
    ]
    tables = ((buo_hbm, buo, BUO), (lame_hbm, lame, MOD), (shear_hbm, shear, MOD))
    mat_loads = [
        pltpu.make_async_copy(source, target.at[pl.ds(lead, DEPTH)], in_sem.at[9 + k])
        for k, (source, target, lead) in enumerate(tables)
    ]
    for copy in loads + mat_loads:
        copy.start()

    zero = jnp.zeros((PAD, COLS), F32)
    plane = jnp.zeros((ROWS, COLS), F32)

    @pl.loop(0, 9)
    def _(part):
        for z in range(DEPTH + 2 * OWN):
            own[part, z, pl.ds(0, PAD), :] = zero
            own[part, z, pl.ds(PAD + ROWS, PAD), :] = zero
        for z in range(DEPTH + 2 * FAR):
            other[part, z, pl.ds(0, PAD), :] = zero
            other[part, z, pl.ds(PAD + ROWS, PAD), :] = zero
        for z in list(range(OWN)) + list(range(OWN + DEPTH, DEPTH + 2 * OWN)):
            own[part, z, inner, :] = plane

    def clear(base_mat, base_own):
        for _, target, lead in tables:
            for z in range(lead):
                target[z + (lead + DEPTH if base_mat else 0)] = plane

        @pl.loop(0, 9)
        def _(part):
            for z in range(FAR):
                got[part, z + base_own] = jnp.zeros((ROWS, COLS), BF16)

    @pl.when(jnp.logical_not(has_down))
    def _():
        clear(0, 0)

    @pl.when(jnp.logical_not(has_up))
    def _():
        clear(1, FAR + DEPTH)

    spread = (
        lax.broadcasted_iota(jnp.int32, (COLS // BLOCK, COLS), 0)
        == lanes((COLS // BLOCK, COLS)) // BLOCK
    ).astype(F32)
    exp_rows[...] = jnp.dot(
        exps[...].astype(F32), spread, preferred_element_type=F32, precision=lax.Precision.HIGHEST
    )

    @pl.loop(0, 9 * ROWS // BLOCK)
    def _(i):
        level = jnp.broadcast_to(exp_rows[pl.ds(i, 1), :], (BLOCK, COLS))
        upscale = jnp.ones((BLOCK, COLS), F32)
        downscale = upscale
        for exponent in (-2, -1, 1, 2):
            chosen = jnp.abs(level - exponent) < 0.5
            upscale = jnp.where(chosen, 2.0**exponent, upscale)
            downscale = jnp.where(chosen, 2.0**-exponent, downscale)
        up_rows[pl.ds(pl.multiple_of(i * BLOCK, BLOCK), BLOCK), :] = upscale
        down_rows[pl.ds(pl.multiple_of(i * BLOCK, BLOCK), BLOCK), :] = downscale

    sums[...] = jnp.zeros_like(sums)

    for copy in loads:
        copy.wait()

    @pl.loop(0, 9)
    def _(part):
        for z in (0, 1, 2, 5, 6, 7):
            mirror[0, part, z] = own[part, z + OWN, inner, :].astype(BF16)

    pl.semaphore_wait(
        barrier, 1 + len(near_peers) + len(wide_peers) + has_up.astype(jnp.int32) + has_down.astype(jnp.int32)
    )

    def halo_up(step):
        return [
            remote(mirror.at[step, pl.ds(0, 6), pl.ds(6, 2)], low_a.at[step],
                   halo_send.at[step, 0, 0], halo_recv.at[step, 0, 0], up),
            remote(mirror.at[step, pl.ds(6, 3), pl.ds(5, 3)], low_b.at[step],
                   halo_send.at[step, 0, 1], halo_recv.at[step, 0, 1], up),
        ]

    def halo_down(step):
        return [
            remote(mirror.at[step, pl.ds(0, 6), pl.ds(0, 2)], high_a.at[step],
                   halo_send.at[step, 1, 0], halo_recv.at[step, 1, 0], down),
            remote(mirror.at[step, pl.ds(6, 3), pl.ds(0, 3)], high_b.at[step],
                   halo_send.at[step, 1, 1], halo_recv.at[step, 1, 1], down),
        ]

    def mat_up():
        return [
            remote(target.at[pl.ds(DEPTH, lead)], target.at[pl.ds(0, lead)],
                   mat_send.at[k, 0], mat_recv.at[k, 0], up)
            for k, (_, target, lead) in enumerate(tables)
        ]

    def mat_down():
        return [
            remote(target.at[pl.ds(lead, lead)], target.at[pl.ds(lead + DEPTH, lead)],
                   mat_send.at[k, 1], mat_recv.at[k, 1], down)
            for k, (_, target, lead) in enumerate(tables)
        ]

    def send_halos(step):
        @pl.when(has_up)
        def _():
            for copy in halo_up(step):
                copy.start()

        @pl.when(has_down)
        def _():
            for copy in halo_down(step):
                copy.start()

    send_halos(0)
    for copy in mat_loads:
        copy.wait()

    @pl.when(has_up)
    def _():
        for copy in mat_up():
            copy.start()

    @pl.when(has_down)
    def _():
        for copy in mat_down():
            copy.start()

    row_parts = list(zip(ROW_CUTS[:-1], ROW_CUTS[1:]))

    def across(index):
        if index == 0:
            layer, count, lo, hi = 3, 2, 0, ROWS
        else:
            lo, hi = row_parts[(index - 1) // 2]
            layer, count = (0, 3) if index % 2 else (5, 3)
        return remote(
            mirror.at[1, :, pl.ds(layer, count), pl.ds(lo, hi - lo)],
            got.at[:, pl.ds(FAR + layer, count), pl.ds(lo, hi - lo)],
            x_send.at[index], x_recv.at[index], partner,
        )

    across_count = 1 + 2 * len(row_parts)

    def forward_up(index):
        if index == 0:
            return [remote(got.at[:, pl.ds(FAR + 3, 2)], got.at[:, pl.ds(1, 2)],
                           fwd_send.at[0, 0, 0], fwd_recv.at[0, 0, 0], up)]
        lo, hi = row_parts[index - 1]
        rows = pl.ds(lo, hi - lo)
        return [
            remote(got.at[:, pl.ds(FAR + 5, 3), rows], got.at[:, pl.ds(3, 3), rows],
                   fwd_send.at[index, 0, 0], fwd_recv.at[index, 0, 0], up),
            remote(got.at[pl.ds(6, 3), pl.ds(FAR + 2, 1), rows], got.at[pl.ds(6, 3), pl.ds(0, 1), rows],
                   fwd_send.at[index, 0, 1], fwd_recv.at[index, 0, 1], up),
        ]

    def forward_down(index):
        base = FAR + DEPTH
        if index == 0:
            return [remote(got.at[:, pl.ds(FAR + 3, 2)], got.at[:, pl.ds(base + 3, 2)],
                           fwd_send.at[0, 1, 0], fwd_recv.at[0, 1, 0], down)]
        lo, hi = row_parts[index - 1]
        rows = pl.ds(lo, hi - lo)
        return [
            remote(got.at[:, pl.ds(FAR, 3), rows], got.at[:, pl.ds(base, 3), rows],
                   fwd_send.at[index, 1, 0], fwd_recv.at[index, 1, 0], down),
            remote(got.at[pl.ds(6, 3), pl.ds(FAR + 5, 1), rows], got.at[pl.ds(6, 3), pl.ds(base + 5, 1), rows],
                   fwd_send.at[index, 1, 1], fwd_recv.at[index, 1, 1], down),
        ]

    def pass_on(index):
        if index == 0:
            across(0).wait_recv()
        else:
            across(2 * index - 1).wait_recv()
            across(2 * index).wait_recv()

        @pl.when(has_up)
        def _():
            for copy in forward_up(index):
                copy.start()

        @pl.when(has_down)
        def _():
            for copy in forward_down(index):
                copy.start()

    def image_of(shot, step):
        def image(z, y):
            cell = (
                ((me * DEPTH + z) * ROWS + y) * COLS
                + lax.broadcasted_iota(jnp.int32, (YB, COLS), 0) * COLS
                + lanes((YB, COLS))
            )
            total = jnp.zeros((YB, COLS), F32)
            for j in range(SOURCES):
                total = total + jnp.where(cell == cells[shot, j], wavelet[shot, step, j], 0.0)
            return total

        return image

    mine = Slab(own, OWN, buo, lame, shear)
    every = (0, ROWS)

    def record(step, count, place):
        def body(k, carry):
            part, z = k // count, place(lax.rem(k, count))
            sizes, misfits, squares = carry
            for y in range(0, ROWS, YB):
                value = mine.at(part, z, y)
                rounded = value.astype(BF16)
                mirror[step + 1, part, z, pl.ds(y, YB), :] = rounded
                at = pl.ds(pl.multiple_of(part * ROWS + y, YB), YB)
                level = jnp.clip(rounded.astype(F32) * down_rows[at, :], -clip_level, clip_level)
                misfit = value - level * up_rows[at, :]
                sizes = sizes + jnp.abs(level)
                misfits = misfits + misfit * misfit
                squares = squares + value * value
            return sizes, misfits, squares

        start = tuple(sums[step, k] for k in range(3))
        for k, total in enumerate(lax.fori_loop(0, 9 * count, body, start)):
            sums[step, k] = total

    edges = lambda first, gap: (lambda i: first + i + (i // 3) * gap)

    @pl.loop(0, STEPS)
    def _(step):
        @pl.when(step > 0)
        def _():
            send_halos(step)

        @pl.when(step == 2)
        def _():
            pass_on(0)

        image = image_of(peer, step)
        run_velocity(mine, 5, lambda i: i + 2, lambda i: i + 1, every)
        middle = (2, lambda i: i + 3)
        run_stress(mine, middle, middle, every, image)
        record(step, *middle)

        @pl.when(step == 0)
        def _():
            across(0).start()

        @pl.when(has_down)
        def _():
            for copy in halo_up(step):
                copy.wait_recv()

            @pl.when(step == 0)
            def _():
                for copy in mat_up():
                    copy.wait_recv()

            @pl.loop(0, 6)
            def _(part):
                for z in range(2):
                    own[part, OWN - 2 + z, inner, :] = low_a[step, part, z].astype(F32)

            @pl.loop(0, 3)
            def _(part):
                for z in range(3):
                    own[part + 6, OWN - 3 + z, inner, :] = low_b[step, part, z].astype(F32)

        @pl.when(has_up)
        def _():
            for copy in halo_down(step):
                copy.wait_recv()

            @pl.when(step == 0)
            def _():
                for copy in mat_down():
                    copy.wait_recv()

            @pl.loop(0, 6)
            def _(part):
                for z in range(2):
                    own[part, OWN + DEPTH + z, inner, :] = high_a[step, part, z].astype(F32)

            @pl.loop(0, 3)
            def _(part):
                for z in range(3):
                    own[part + 6, OWN + DEPTH + z, inner, :] = high_b[step, part, z].astype(F32)

        run_velocity(mine, 6, edges(-1, 5), edges(-2, 5), every)
        outer = (6, edges(0, 2))
        run_stress(mine, outer, outer, every, image)
        record(step, *outer)

        @pl.when(step == 0)
        def _():
            for index in range(1, across_count):
                across(index).start()

    store_final = pltpu.make_async_copy(
        own.at[:, pl.ds(OWN, DEPTH), inner, :], final_hbm.at[0], out_sem.at[0]
    )
    store_final.start()

    row8 = lax.broadcasted_iota(jnp.int32, (8, COLS), 0)
    lane8 = lanes((8, COLS))
    tile = jnp.zeros((8, COLS), F32)
    for step in range(STEPS):
        for k in range(3):
            tile = tile + jnp.where((row8 == step) & (lane8 == k), jnp.sum(sums[step, k]), 0.0)

    def gather(phase, peers, mine_at, size, tile):
        stat_src[phase] = tile
        copies = [
            remote(stat_src.at[phase], stat_rx.at[phase, mine_at],
                   stat_send.at[phase, k], stat_recv.at[phase, k], device)
            for k, device in enumerate(peers)
        ]
        for copy in copies:
            copy.start()
        stat_rx[phase, mine_at] = tile
        for copy in copies:
            copy.wait()
        total = stat_rx[phase, 0]
        for k in range(1, size):
            total = total + stat_rx[phase, k]
        return total

    tile = gather(0, near_peers, lane_of, LOW, tile)
    tile = gather(1, wide_peers, block, groups, tile)
    scaled = tile * (1.0 / (9 * slabs * DEPTH * ROWS * COLS))
    ratio = pltpu.roll(scaled, COLS - 1, 1) / (pltpu.roll(scaled, COLS - 2, 1) + energy_floor)
    table = jnp.where(lane8 == 0, scaled, pltpu.roll(jnp.sqrt(ratio), 1, 1))
    stats_out[...] = table[:STEPS, :2]

    theirs = Slab(other, FAR, buo, lame, shear)

    def widen(rows):
        lo, hi = rows

        @pl.loop(0, 9)
        def _(part):
            @pl.loop(1, DEPTH + 2 * FAR - 1)
            def _(z):
                other[part, z, pl.ds(PAD + lo, hi - lo), :] = got[part, z, pl.ds(lo, hi - lo), :].astype(F32)

        @pl.loop(6, 9)
        def _(part):
            for z in (0, DEPTH + 2 * FAR - 1):
                other[part, z, pl.ds(PAD + lo, hi - lo), :] = got[part, z, pl.ds(lo, hi - lo), :].astype(F32)

    def compress(step, rows):
        lo, hi = rows

        @pl.loop(0, 9)
        def _(part):
            @pl.loop(0, DEPTH)
            def _(z):
                for y in range(lo // YB * YB, hi, YB):
                    at = pl.ds(pl.multiple_of(part * ROWS + y, YB), YB)
                    level = jnp.clip(theirs.at(part, z, y) * down_rows[at, :], -clip_level, clip_level)
                    if lo > y or hi < y + YB:
                        row = lax.broadcasted_iota(jnp.int32, (YB, COLS), 0) + y
                        before = packed[step, part, z, pl.ds(y, YB), :].astype(F32)
                        level = jnp.where((row >= lo) & (row < hi), level, before)
                    packed[step, part, z, pl.ds(y, YB), :] = level.astype(BF16)

    stores = []

    def store_payload(step, index, rows):
        lo, hi = (bound // YB * YB for bound in rows)
        if lo < hi:
            stores.append(
                pltpu.make_async_copy(
                    packed.at[step, :, :, pl.ds(lo, hi - lo)],
                    stored_hbm.at[0, step, :, :, pl.ds(lo, hi - lo)],
                    out_sem.at[1 + step * len(row_parts) + index],
                )
            )
            stores[-1].start()

    for index in range(1, len(row_parts) + 1):
        pass_on(index)

    last = len(row_parts) - 1
    done = [0, 0, 0, 0]
    for index, (lo, hi) in enumerate(row_parts):
        @pl.when(has_down)
        def _():
            for copy in (forward_up(0) if index == 0 else []) + forward_up(index + 1):
                copy.wait_recv()

        @pl.when(has_up)
        def _():
            for copy in (forward_down(0) if index == 0 else []) + forward_down(index + 1):
                copy.wait_recv()

        widen((lo, hi))
        compress(0, (lo, hi))
        store_payload(0, index, (lo, hi))
        ends = [ROWS if index == last else hi - 2 * (k + 1) for k in range(4)]
        spans = list(zip(done, ends))
        run_velocity(theirs, 17, lambda i: i - 4, lambda i: i - 5, spans[0])
        run_stress(theirs, (14, lambda i: i - 3), (11, lambda i: i - 1), spans[1], image_of(1 - peer, 1))
        compress(1, spans[1])
        store_payload(1, index, spans[1])
        run_velocity(theirs, 11, lambda i: i - 1, lambda i: i - 2, spans[2])
        plain = (DEPTH, lambda i: i)
        run_stress(theirs, plain, plain, spans[3], image_of(1 - peer, 2))
        compress(2, spans[3])
        store_payload(2, index, spans[3])
        done = ends

    for index in range(across_count):
        across(index).wait_send()

    @pl.when(has_up)
    def _():
        for copy in mat_up():
            copy.wait_send()
        for step in range(STEPS):
            for copy in halo_up(step):
                copy.wait_send()
        for index in range(len(row_parts) + 1):
            for copy in forward_up(index):
                copy.wait_send()

    @pl.when(has_down)
    def _():
        for copy in mat_down():
            copy.wait_send()
        for step in range(STEPS):
            for copy in halo_down(step):
                copy.wait_send()
        for index in range(len(row_parts) + 1):
            for copy in forward_down(index):
                copy.wait_send()

    store_final.wait()
    for copy in stores:
        copy.wait()


def per_device(slabs, wavefield, buoyancy, lame_lambda, shear_modulus, scale_exponents, source_cells, wavelet):
    hbm = pl.BlockSpec(memory_space=pl.ANY)
    vmem = pl.BlockSpec(memory_space=pltpu.VMEM)
    smem = pl.BlockSpec(memory_space=pltpu.SMEM)
    parts = len(ROW_CUTS) - 1
    dma = pltpu.SemaphoreType.DMA
    final, stored, statistics = pl.pallas_call(
        functools.partial(kernel, slabs),
        out_shape=(
            jax.ShapeDtypeStruct(wavefield.shape, F32),
            jax.ShapeDtypeStruct((1, STEPS, 9, DEPTH, ROWS, COLS), BF16),
            jax.ShapeDtypeStruct((STEPS, 2), F32),
        ),
        in_specs=[hbm, hbm, hbm, hbm, vmem, smem, smem],
        out_specs=(hbm, hbm, vmem),
        scratch_shapes=[
            pltpu.VMEM((9, DEPTH + 2 * OWN, ROWS + 2 * PAD, COLS), F32),
            pltpu.VMEM((9, DEPTH + 2 * FAR, ROWS + 2 * PAD, COLS), F32),
            pltpu.VMEM((STEPS + 1, 9, DEPTH, ROWS, COLS), BF16),
            pltpu.VMEM((STEPS, 6, 2, ROWS, COLS), BF16),
            pltpu.VMEM((STEPS, 3, 3, ROWS, COLS), BF16),
            pltpu.VMEM((STEPS, 6, 2, ROWS, COLS), BF16),
            pltpu.VMEM((STEPS, 3, 3, ROWS, COLS), BF16),
            pltpu.VMEM((DEPTH + 2 * BUO, ROWS, COLS), F32),
            pltpu.VMEM((DEPTH + 2 * MOD, ROWS, COLS), F32),
            pltpu.VMEM((DEPTH + 2 * MOD, ROWS, COLS), F32),
            pltpu.VMEM((9, DEPTH + 2 * FAR, ROWS, COLS), BF16),
            pltpu.VMEM((STEPS, 9, DEPTH, ROWS, COLS), BF16),
            pltpu.VMEM((9 * ROWS, COLS), F32),
            pltpu.VMEM((9 * ROWS, COLS), F32),
            pltpu.VMEM((9 * ROWS // BLOCK, COLS), F32),
            pltpu.VMEM((STEPS, 3, YB, COLS), F32),
            pltpu.VMEM((2, 8, COLS), F32),
            pltpu.VMEM((2, max(LOW, slabs // LOW), 8, COLS), F32),
            dma((12,)),
            dma((1 + STEPS * parts,)),
            dma((STEPS, 2, 2)),
            dma((STEPS, 2, 2)),
            dma((3, 2)),
            dma((3, 2)),
            dma((1 + 2 * parts,)),
            dma((1 + 2 * parts,)),
            dma((1 + parts, 2, 2)),
            dma((1 + parts, 2, 2)),
            dma((2, max(LOW, slabs // LOW))),
            dma((2, max(LOW, slabs // LOW))),
        ],
        compiler_params=pltpu.CompilerParams(
            collective_id=0, has_side_effects=True, vmem_limit_bytes=60 * 1024 * 1024
        ),
        name="elastic_steps",
    )(
        wavefield, buoyancy, lame_lambda, shear_modulus,
        scale_exponents.reshape(9 * ROWS // BLOCK, COLS // BLOCK), source_cells, wavelet,
    )
    return final, stored, statistics[None]


def solution(mesh):
    return jax.shard_map(
        functools.partial(per_device, mesh.shape["space"]),
        mesh=mesh,
        in_specs=(
            P("peer", None, "space", None, None),
            P("space", None, None),
            P("space", None, None),
            P("space", None, None),
            P(None, "space", None, None),
            P(),
            P(),
        ),
        out_specs=(
            P("peer", None, "space", None, None),
            P("peer", None, None, "space", None, None),
            P("peer", None, None),
        ),
        check_vma=False,
    )
```

time: 194 us -> 143 us (0.74)
  Pallas kernels: 0 us -> 133 us
  starting transfers between devices: 65.8 us -> 0 us
  blocking collectives: 65 us -> 0 us
  other arithmetic: 31.9 us -> 0 us
  local copies, waits for them, and re-layouts: 18.6 us -> 7.88 us
  waiting for transfers between devices: 10.4 us -> 0 us
    pallas_call x0 -> x1, Pallas kernels: none -> 133 us  [per_device(): pl.pallas_call(functools.partial(kernel, slabs), out_shape=(jax.ShapeDtyp...]
    ppermute x15 -> x0, starting transfers between devices: 65.8 us -> none  [the longest x6 47.7 us: extended(): lax.ppermute(head, axis, [((i + 1) % count, i) for i in range(ends)])]
    all_to_all x1 -> x0, blocking collectives: 65 us -> none  [copy_for_each(): lax.all_to_all(jnp.broadcast_to(array[None], (count, *array.shape)), axis...]
    another operation x25 -> x0, other arithmetic: 10.7 us -> none  [the longest x4 5.94 us: per_device(): totals = over_copies(jnp.stack(local_sums, axis=0), 'space')]
    ppermute x15 -> x0, waiting for transfers between devices: 10.4 us -> none  [the longest x6 9.17 us: extended(): lax.ppermute(head, axis, [((i + 1) % count, i) for i in range(ends)])]
    eq x14 -> x0, local copies, waits for them, and re-layouts: 8.55 us -> none  [scale_tables(): chosen = expanded == exponent]
    unnamed x41 -> x5, local copies, waits for them, and re-layouts: 1.18 us -> 6.58 us
    select_n x8 -> x0, local copies, waits for them, and re-layouts: 5.15 us -> none  [the longest x4 4.03 us: scale_tables(): upscale = jnp.where(chosen, jnp.float32(2.0 ** exponent), upscale)]
  transfers between devices with their start and end apart: 15 -> 0, of which waited for: 10 -> 0; matrix products, arithmetic and copies ran while one was open for 16% -> 0% of each run, Pallas kernels for 0% -> 0%
where the time goes in v1:
time: 143 us; the launch traced here: 142 us
  Pallas kernels  133 us (93%)
  local copies, waits for them, and re-layouts  7.88 us (6%)
    pallas_call x1, Pallas kernels, per_device(): pl.pallas_call(functools.partial(kernel, slabs), out_shape=(jax.ShapeDtyp...  133 us
    unnamed x5, local copies, waits for them, and re-layouts  6.58 us

profile of v1, /device:TPU:2, one launch (start us, length us, event | category | flops | bytes accessed | tf_op | source)
XLA Modules:
  0.0 141.8 jit_solution(9145725383008925979)
XLA Ops:
  0.6 1.3 copy.10.wavelet
  1.9 133.2 %elastic_steps.1 = (f32[1,9,8,64,128]{4,3,2,1,0:T(8,128)}, bf16[1,3,9,8,64,128]{5,4,3,2,1,0:T(8,128)(2,1)}, f32[3,2]{1,0:T(4,128)}) custom-call(f32[1,9,8,64,128]{4,3,2,1,0:T(8,128)} %wave_hbm.1, f32[8,64,128]{2,1,0:T(8,128)} %buo_hbm.1, f32[8,64,128]{2,1,0:T(8,128)} %lame_hbm.1, f32[8,64,128]{2,1,0:T(8,128)} %shear_hbm.1, s32[72,16]{1,0:T(8,128)} %bitcast.2, ...), custom_call_target="tpu_custom_call" | custom-call | tf_op jit(solution)/shard_map/elastic_steps/pallas_call | solution.py:636
  135.2 1.3 copy.11
  136.5 0.0 copy-start
  136.5 3.5 %copy.14 = f32[1,9,8,64,128]{4,3,2,1,0:T(8,128)} copy(f32[1,9,8,64,128]{4,3,2,1,0:T(8,128)} %get-tuple-element.12) | data formatting | bytes 4718592
  140.0 0.0 copy-done
  140.0 1.8 %copy.15 = bf16[1,3,9,8,64,128]{5,4,3,2,1,0:T(8,128)(2,1)} copy(bf16[1,3,9,8,64,128]{5,4,3,2,1,0:T(8,128)(2,1)S(1)} %copy-done) | data formatting | bytes 7077888
Async XLA Ops:
  136.5 3.5 %copy-start = (bf16[1,3,9,8,64,128]{5,4,3,2,1,0:T(8,128)(2,1)S(1)}, bf16[1,3,9,8,64,128]{5,4,3,2,1,0:T(8,128)(2,1)}, u32[]{:S(2)}) copy-start(bf16[1,3,9,8,64,128]{5,4,3,2,1,0:T(8,128)(2,1)} %get-tuple-element.13) | copy-start | bytes 10616836

commit v2 on v1

v2 whole, which is shorter than its diff:
```python
import functools

import jax
import jax.numpy as jnp
from jax import lax
from jax.experimental import pallas as pl
from jax.experimental.pallas import tpu as pltpu
from jax.sharding import PartitionSpec as P

MESH = pl.DeviceIdType.MESH
F32 = jnp.float32
BF16 = jnp.bfloat16

BLOCK = 8
STEPS = 3
SOURCES = 8
DEPTH, ROWS, COLS = 8, 64, 128
PAD = 8
YB = 16
GROUP = 2
MATMUL_X = False
OWN = 3
FAR = 6
BUO, MOD = 5, 3
LOW = 8
ROW_CUTS = (0, 32, 48, 64)
VX, VY, VZ, SXX, SYY, SXY, SZZ, SXZ, SYZ = range(9)
clip_level = 4.0
energy_floor = 1e-06


def lanes(shape):
    return lax.broadcasted_iota(jnp.int32, shape, 1)


class Slab:
    def __init__(self, ref, lead, buoyancy, lame, shear, band):
        self.ref, self.lead = ref, lead
        self.buoyancy, self.lame, self.shear, self.band = buoyancy, lame, shear, band

    def rows(self, rows):
        self.lo, self.hi = rows
        self.y = self.lo // BLOCK * BLOCK
        self.n = -(-self.hi // BLOCK) * BLOCK - self.y
        return self

    def at(self, part, z):
        return self.ref[part, z + self.lead, pl.ds(self.y + PAD, self.n), :]

    def put(self, part, z, value):
        ref, n = self.ref, self.n
        head = BLOCK if self.lo % BLOCK else 0
        tail = BLOCK if self.hi % BLOCK else 0
        row = lax.broadcasted_iota(jnp.int32, (BLOCK, COLS), 0)
        if head:
            at = pl.ds(self.y + PAD, BLOCK)
            keep = row >= self.lo % BLOCK
            if n == BLOCK and tail:
                keep = keep & (row < self.hi % BLOCK)
                tail = 0
            ref[part, z + self.lead, at, :] = jnp.where(keep, value[:BLOCK], ref[part, z + self.lead, at, :])
        if tail:
            at = pl.ds(self.y + PAD + n - BLOCK, BLOCK)
            keep = row < self.hi % BLOCK
            ref[part, z + self.lead, at, :] = jnp.where(
                keep, value[n - BLOCK :], ref[part, z + self.lead, at, :]
            )
        if n - head - tail:
            ref[part, z + self.lead, pl.ds(self.y + PAD + head, n - head - tail), :] = value[head : n - tail]


    def dx(self, part, z, forward):
        f = self.at(part, z)
        if self.band is not None:
            top = f.astype(BF16)
            rest = (f - top.astype(F32)).astype(BF16)
            return jnp.dot(
                jnp.concatenate([top, rest], axis=1), self.band[int(forward)], preferred_element_type=F32
            )
        lane = lanes((1, COLS))
        after = jnp.where(lane < COLS - 1, pltpu.roll(f, COLS - 1, 1), 0.0)
        before = jnp.where(lane >= 1, pltpu.roll(f, 1, 1), 0.0)
        if forward:
            far = jnp.where(lane < COLS - 2, pltpu.roll(f, COLS - 2, 1), 0.0)
            return 27.0 * (after - f) - (far - before)
        far = jnp.where(lane >= 2, pltpu.roll(f, 2, 1), 0.0)
        return 27.0 * (f - before) - (after - far)

    def dy(self, part, z, forward):
        window = self.ref[part, z + self.lead, pl.ds(self.y, self.n + 2 * PAD), :]
        get = lambda shift: window[PAD + shift : PAD + shift + self.n]
        if forward:
            return get(1) - get(0), get(2) - get(-1)
        return get(0) - get(-1), get(1) - get(-2)

    def dz(self, part, z, forward):
        get = lambda shift: self.at(part, z + shift)
        if forward:
            return get(1) - get(0), get(2) - get(-1)
        return get(0) - get(-1), get(1) - get(-2)

    def mat(self, table, lead, z, factor):
        return table[z + lead, pl.ds(self.y, self.n), :] * factor

    def velocity(self, zs):
        results = []
        for z in zs:
            for part, along_x, along_y, along_z, at in (
                (VX, (SXX, True), (SXY, False), (SXZ, False), z),
                (VY, (SXY, False), (SYY, True), (SYZ, False), z),
                (VZ, (SXZ, False), (SYZ, False), (SZZ, True), z - 1),
            ):
                x = self.dx(along_x[0], at, along_x[1])
                y = self.dy(along_y[0], at, along_y[1])
                d = self.dz(along_z[0], at, along_z[1])
                change = 27.0 * (y[0] + d[0]) - (y[1] + d[1]) + x
                value = self.at(part, at) + self.mat(self.buoyancy, BUO, at, 1.0 / 24.0) * change
                results.append((part, at, value))
        for part, at, value in results:
            self.put(part, at, value)

    def stress(self, zs, image, plane_shear=True):
        results = []
        for z in zs:
            join = lambda pair: 27.0 * pair[0] - pair[1]
            strain = (
                self.dx(VX, z, False), join(self.dy(VY, z, False)), join(self.dz(VZ, z, False)),
            )
            shear = self.mat(self.shear, MOD, z, 1.0 / 24.0)
            pressure = self.mat(self.lame, MOD, z, 1.0 / 24.0) * (
                strain[0] + strain[1] + strain[2]
            ) + image(z, self.y, self.n)
            double = shear + shear
            for part, value in zip((SXX, SYY, SZZ), strain):
                results.append((part, z, self.at(part, z) + (pressure + double * value)))
            if plane_shear:
                change = join(self.dy(VX, z, True)) + self.dx(VY, z, True)
                results.append((SXY, z, self.at(SXY, z) + shear * change))
            change = join(self.dz(VX, z, True)) + self.dx(VZ, z, True)
            results.append((SXZ, z, self.at(SXZ, z) + shear * change))
            y, d = self.dy(VZ, z, True), self.dz(VY, z, True)
            change = 27.0 * (y[0] + d[0]) - (y[1] + d[1])
            results.append((SYZ, z, self.at(SYZ, z) + shear * change))
        for part, at, value in results:
            self.put(part, at, value)


def over(count, place, group, body):
    @pl.loop(0, count // group)
    def _(i):
        body([place(i * group + k) for k in range(group)])

    if count % group:
        body([place(i) for i in range(count // group * group, count)])


def kernel(
    slabs,
    wave_hbm, buo_hbm, lame_hbm, shear_hbm, exps, cells, wavelet,
    final_hbm, stored_hbm, stats_out,
    own, other, mirror, low_a, low_b, high_a, high_b, buo, lame, shear, got, packed,
    up_rows, down_rows, exp_rows, sums, stat_src, stat_rx,
    in_sem, out_sem, halo_send, halo_recv, mat_send, mat_recv,
    x_send, x_recv, fwd_send, fwd_recv, stat_send, stat_recv, *extra,
):
    me, peer = lax.axis_index("space"), lax.axis_index("peer")
    has_down, has_up = me > 0, me < slabs - 1
    up, down = (me + 1, peer), (me - 1, peer)
    partner = (me, 1 - peer)
    half = slabs // 2
    below_cross, above_cross = me == half - 1, me == half
    cross_up, cross_down = (me + 1, 1 - peer), (me - 1, 1 - peer)
    groups = slabs // LOW
    block, lane_of = me // LOW, lax.rem(me, LOW)
    near_peers = [(block * LOW + lax.rem(lane_of + k, LOW), peer) for k in range(1, LOW)]
    wide_peers = [(lax.rem(block + k, groups) * LOW + lane_of, peer) for k in range(1, groups)]

    barrier = pltpu.get_barrier_semaphore()
    for device in [partner] + near_peers + wide_peers:
        pl.semaphore_signal(barrier, inc=1, device_id=device, device_id_type=MESH)

    @pl.when(has_up)
    def _():
        pl.semaphore_signal(barrier, inc=1, device_id=up, device_id_type=MESH)

    @pl.when(has_down)
    def _():
        pl.semaphore_signal(barrier, inc=1, device_id=down, device_id_type=MESH)

    @pl.when(below_cross)
    def _():
        pl.semaphore_signal(barrier, inc=1, device_id=cross_up, device_id_type=MESH)

    @pl.when(above_cross)
    def _():
        pl.semaphore_signal(barrier, inc=1, device_id=cross_down, device_id_type=MESH)

    def remote(source, target, send, recv, device):
        return pltpu.make_async_remote_copy(
            src_ref=source, dst_ref=target, send_sem=send, recv_sem=recv,
            device_id=device, device_id_type=MESH,
        )

    inner = pl.ds(PAD, ROWS)
    loads = [
        pltpu.make_async_copy(
            wave_hbm.at[0, part], own.at[part, pl.ds(OWN, DEPTH), inner, :], in_sem.at[part]
        )
        for part in range(9)
    ]
    tables = ((buo_hbm, buo, BUO), (lame_hbm, lame, MOD), (shear_hbm, shear, MOD))
    mat_loads = [
        pltpu.make_async_copy(source, target.at[pl.ds(lead, DEPTH)], in_sem.at[9 + k])
        for k, (source, target, lead) in enumerate(tables)
    ]
    for copy in loads + mat_loads:
        copy.start()

    zero = jnp.zeros((PAD, COLS), F32)
    plane = jnp.zeros((ROWS, COLS), F32)

    @pl.loop(0, 9)
    def _(part):
        for z in range(DEPTH + 2 * OWN):
            own[part, z, pl.ds(0, PAD), :] = zero
            own[part, z, pl.ds(PAD + ROWS, PAD), :] = zero
        for z in list(range(OWN)) + list(range(OWN + DEPTH, DEPTH + 2 * OWN)):
            own[part, z, inner, :] = plane

    def clear(base_mat, base_own):
        for _, target, lead in tables:
            for z in range(lead):
                target[z + (lead + DEPTH if base_mat else 0)] = plane

        @pl.loop(0, 9)
        def _(part):
            for z in range(FAR):
                got[part, z + base_own] = jnp.zeros((ROWS, COLS), BF16)

    @pl.when(jnp.logical_not(has_down))
    def _():
        clear(0, 0)

    @pl.when(jnp.logical_not(has_up))
    def _():
        clear(1, FAR + DEPTH)

    sums[...] = jnp.zeros_like(sums)

    for copy in loads:
        copy.wait()

    @pl.loop(0, 9)
    def _(part):
        for z in (0, 1, 2, 5, 6, 7):
            mirror[0, part, z] = own[part, z + OWN, inner, :].astype(BF16)

    greeted = [flag.astype(jnp.int32) for flag in (has_up, has_down, below_cross, above_cross)]
    pl.semaphore_wait(barrier, 1 + len(near_peers) + len(wide_peers) + sum(greeted))

    def halo_up(step):
        return [
            remote(mirror.at[step, pl.ds(0, 6), pl.ds(6, 2)], low_a.at[step],
                   halo_send.at[step, 0, 0], halo_recv.at[step, 0, 0], up),
            remote(mirror.at[step, pl.ds(6, 3), pl.ds(5, 3)], low_b.at[step],
                   halo_send.at[step, 0, 1], halo_recv.at[step, 0, 1], up),
        ]

    def halo_down(step):
        return [
            remote(mirror.at[step, pl.ds(0, 6), pl.ds(0, 2)], high_a.at[step],
                   halo_send.at[step, 1, 0], halo_recv.at[step, 1, 0], down),
            remote(mirror.at[step, pl.ds(6, 3), pl.ds(0, 3)], high_b.at[step],
                   halo_send.at[step, 1, 1], halo_recv.at[step, 1, 1], down),
        ]

    def mat_up():
        return [
            remote(target.at[pl.ds(DEPTH, lead)], target.at[pl.ds(0, lead)],
                   mat_send.at[k, 0], mat_recv.at[k, 0], up)
            for k, (_, target, lead) in enumerate(tables)
        ]

    def mat_down():
        return [
            remote(target.at[pl.ds(lead, lead)], target.at[pl.ds(lead + DEPTH, lead)],
                   mat_send.at[k, 1], mat_recv.at[k, 1], down)
            for k, (_, target, lead) in enumerate(tables)
        ]

    def send_halos(step):
        @pl.when(has_up)
        def _():
            for copy in halo_up(step):
                copy.start()

        @pl.when(has_down)
        def _():
            for copy in halo_down(step):
                copy.start()

    send_halos(0)
    for copy in mat_loads:
        copy.wait()

    @pl.when(has_up)
    def _():
        for copy in mat_up():
            copy.start()

    @pl.when(has_down)
    def _():
        for copy in mat_down():
            copy.start()

    spread = (
        lax.broadcasted_iota(jnp.int32, (COLS // BLOCK, COLS), 0)
        == lanes((COLS // BLOCK, COLS)) // BLOCK
    ).astype(F32)
    exp_rows[...] = jnp.dot(
        exps[...].astype(F32), spread, preferred_element_type=F32, precision=lax.Precision.HIGHEST
    )

    @pl.loop(0, 9 * ROWS // BLOCK)
    def _(i):
        level = jnp.broadcast_to(exp_rows[pl.ds(i, 1), :], (BLOCK, COLS))
        upscale = jnp.ones((BLOCK, COLS), F32)
        downscale = upscale
        for exponent in (-2, -1, 1, 2):
            chosen = jnp.abs(level - exponent) < 0.5
            upscale = jnp.where(chosen, 2.0**exponent, upscale)
            downscale = jnp.where(chosen, 2.0**-exponent, downscale)
        up_rows[pl.ds(pl.multiple_of(i * BLOCK, BLOCK), BLOCK), :] = upscale
        down_rows[pl.ds(pl.multiple_of(i * BLOCK, BLOCK), BLOCK), :] = downscale

    @pl.loop(0, 9)
    def _(part):
        for z in range(DEPTH + 2 * FAR):
            other[part, z, pl.ds(0, PAD), :] = zero
            other[part, z, pl.ds(PAD + ROWS, PAD), :] = zero

    band = extra[0] if MATMUL_X else None
    if MATMUL_X:
        row = lax.broadcasted_iota(jnp.int32, (2 * COLS, COLS), 0)
        offset = lax.rem(row, COLS) - lanes((2 * COLS, COLS))
        for k, sign in ((0, -1), (1, 1)):
            weight = jnp.where(offset == 0, -27.0 * sign, 0.0)
            weight = jnp.where(offset == sign, 27.0 * sign, weight)
            weight = jnp.where(offset == -sign, 1.0 * sign, weight)
            weight = jnp.where(offset == 2 * sign, -1.0 * sign, weight)
            band[k] = weight.astype(BF16)

    row_parts = list(zip(ROW_CUTS[:-1], ROW_CUTS[1:]))

    def across(index):
        if index == 0:
            layer, count, lo, hi = 3, 2, 0, ROWS
        else:
            lo, hi = row_parts[(index - 1) // 2]
            layer, count = (0, 3) if index % 2 else (5, 3)
        return remote(
            mirror.at[1, :, pl.ds(layer, count), pl.ds(lo, hi - lo)],
            got.at[:, pl.ds(FAR + layer, count), pl.ds(lo, hi - lo)],
            x_send.at[index], x_recv.at[index], partner,
        )

    across_count = 1 + 2 * len(row_parts)

    def forward(index, source, lead, upward, device):
        side, base = (0, 0) if upward else (1, FAR + DEPTH)
        if index == 0:
            return [
                remote(source.at[:, pl.ds(lead + 3, 2)], got.at[:, pl.ds(base + (1 if upward else 3), 2)],
                       fwd_send.at[0, side, 0], fwd_recv.at[0, side, 0], device)
            ]
        lo, hi = row_parts[index - 1]
        rows, deep = pl.ds(lo, hi - lo), pl.ds(6, 3)
        first, single = (5, 2) if upward else (0, 5)
        return [
            remote(source.at[:, pl.ds(lead + first, 3), rows],
                   got.at[:, pl.ds(base + (3 if upward else 0), 3), rows],
                   fwd_send.at[index, side, 0], fwd_recv.at[index, side, 0], device),
            remote(source.at[deep, pl.ds(lead + single, 1), rows],
                   got.at[deep, pl.ds(base + (0 if upward else 5), 1), rows],
                   fwd_send.at[index, side, 1], fwd_recv.at[index, side, 1], device),
        ]

    def forward_up(index):
        return forward(index, got, FAR, True, up)

    def forward_down(index):
        return forward(index, got, FAR, False, down)

    def straight_up(index):
        return forward(index, mirror.at[1], 0, True, cross_up)

    def straight_down(index):
        return forward(index, mirror.at[1], 0, False, cross_down)

    def each(flag, copies, act):
        @pl.when(flag)
        def _():
            for copy in copies():
                act(copy)

    begin, sent = (lambda copy: copy.start()), (lambda copy: copy.wait_send())
    passes_up = has_up & jnp.logical_not(below_cross)
    passes_down = has_down & jnp.logical_not(above_cross)

    def pass_on(index):
        if index == 0:
            across(0).wait_recv()
        else:
            across(2 * index - 1).wait_recv()
            across(2 * index).wait_recv()
        each(passes_up, lambda: forward_up(index), begin)
        each(passes_down, lambda: forward_down(index), begin)

    def send_across(index):
        if index == 0:
            across(0).start()
        else:
            across(2 * index - 1).start()
            across(2 * index).start()
        each(below_cross, lambda: straight_up(index), begin)
        each(above_cross, lambda: straight_down(index), begin)

    def image_of(shot, step):
        def image(z, y, n):
            first = ((me * DEPTH + z) * ROWS + y) * COLS
            place = lax.broadcasted_iota(jnp.int32, (n, COLS), 0) * COLS + lanes((n, COLS))
            total = jnp.zeros((n, COLS), F32)
            for j in range(SOURCES):
                total = total + jnp.where(place == cells[shot, j] - first, wavelet[step, shot, j], 0.0)
            return total

        return image

    mine = Slab(own, OWN, buo, lame, shear, band).rows((0, ROWS))

    def record(step, count, place):
        def body(k, carry):
            part = k // (count // 2)
            down = down_rows[pl.ds(pl.multiple_of(part * ROWS, ROWS), ROWS), :]
            up_scale = up_rows[pl.ds(pl.multiple_of(part * ROWS, ROWS), ROWS), :]
            sizes, misfits, squares = carry
            for half in range(2):
                z = place(lax.rem(k, count // 2) * 2 + half)
                value = mine.at(part, z)
                rounded = value.astype(BF16)
                mirror[step + 1, part, z] = rounded
                level = jnp.clip(rounded.astype(F32) * down, -clip_level, clip_level)
                misfit = value - level * up_scale
                for y in range(0, ROWS, YB):
                    at = slice(y, y + YB)
                    sizes = sizes + jnp.abs(level[at])
                    misfits = misfits + misfit[at] * misfit[at]
                    squares = squares + value[at] * value[at]
            return sizes, misfits, squares

        start = tuple(sums[step, k] for k in range(3))
        for k, total in enumerate(lax.fori_loop(0, 9 * (count // 2), body, start)):
            sums[step, k] = total

    edges = lambda first, gap: (lambda i: first + i + (i // 3) * gap)

    @pl.loop(0, STEPS)
    def _(step):
        @pl.when(step == 2)
        def _():
            pass_on(0)

        image = image_of(peer, step)
        over(5, lambda i: i + 2, GROUP, mine.velocity)
        middle = (2, lambda i: i + 3)
        over(*middle, GROUP, lambda zs: mine.stress(zs, image))
        record(step, *middle)

        @pl.when(step == 0)
        def _():
            send_across(0)

        @pl.when(has_down)
        def _():
            for copy in halo_up(step):
                copy.wait_recv()

            @pl.when(step == 0)
            def _():
                for copy in mat_up():
                    copy.wait_recv()

            @pl.loop(0, 6)
            def _(part):
                for z in range(2):
                    own[part, OWN - 2 + z, inner, :] = low_a[step, part, z].astype(F32)

            @pl.loop(0, 3)
            def _(part):
                for z in range(3):
                    own[part + 6, OWN - 3 + z, inner, :] = low_b[step, part, z].astype(F32)

        @pl.when(has_up)
        def _():
            for copy in halo_down(step):
                copy.wait_recv()

            @pl.when(step == 0)
            def _():
                for copy in mat_down():
                    copy.wait_recv()

            @pl.loop(0, 6)
            def _(part):
                for z in range(2):
                    own[part, OWN + DEPTH + z, inner, :] = high_a[step, part, z].astype(F32)

            @pl.loop(0, 3)
            def _(part):
                for z in range(3):
                    own[part + 6, OWN + DEPTH + z, inner, :] = high_b[step, part, z].astype(F32)

        over(6, edges(-1, 5), GROUP, mine.velocity)
        outer = (6, edges(0, 2))
        over(*outer, GROUP, lambda zs: mine.stress(zs, image))
        record(step, *outer)

        @pl.when(step < STEPS - 1)
        def _():
            send_halos(step + 1)

        @pl.when(step == 0)
        def _():
            send_across(1)

        @pl.when(step == 1)
        def _():
            for index in range(2, len(row_parts) + 1):
                send_across(index)

    store_final = pltpu.make_async_copy(
        own.at[:, pl.ds(OWN, DEPTH), inner, :], final_hbm.at[0], out_sem.at[0]
    )
    store_final.start()

    row8 = lax.broadcasted_iota(jnp.int32, (8, COLS), 0)
    lane8 = lanes((8, COLS))
    tile = jnp.zeros((8, COLS), F32)
    for step in range(STEPS):
        for k in range(3):
            tile = tile + jnp.where((row8 == k) & (lane8 == step), jnp.sum(sums[step, k]), 0.0)

    def gather(phase, peers, mine_at, size, tile):
        stat_src[phase] = tile
        copies = [
            remote(stat_src.at[phase], stat_rx.at[phase, mine_at],
                   stat_send.at[phase, k], stat_recv.at[phase, k], device)
            for k, device in enumerate(peers)
        ]
        for copy in copies:
            copy.start()
        stat_rx[phase, mine_at] = tile
        for copy in copies:
            copy.wait()
        total = stat_rx[phase, 0]
        for k in range(1, size):
            total = total + stat_rx[phase, k]
        return total

    tile = gather(0, near_peers, lane_of, LOW, tile)
    tile = gather(1, wide_peers, block, groups, tile)
    scaled = tile * (1.0 / (9 * slabs * DEPTH * ROWS * COLS))
    ratio = scaled[1:2] / (scaled[2:3] + energy_floor)
    stats_out[0:1, :] = scaled[0:1, :STEPS]
    stats_out[1:2, :] = jnp.sqrt(ratio)[:, :STEPS]

    theirs = Slab(other, FAR, buo, lame, shear, band)

    def widen(rows):
        lo, hi = rows

        def move(part, z):
            other[part, z, pl.ds(PAD + lo, hi - lo), :] = got[part, z, pl.ds(lo, hi - lo), :].astype(F32)

        @pl.loop(0, 9)
        def _(part):
            for z in range(1, DEPTH + 2 * FAR - 1):
                move(part, z)

        for part in range(6, 9):
            for z in (0, DEPTH + 2 * FAR - 1):
                move(part, z)

    def compress(step, rows):
        lo, hi = rows

        @pl.loop(0, 9)
        def _(part):
            for y in range(lo // YB * YB, hi, YB):
                row = lax.broadcasted_iota(jnp.int32, (YB, COLS), 0) + y
                down = down_rows[pl.ds(pl.multiple_of(part * ROWS + y, YB), YB), :]
                for z in range(DEPTH):
                    value = other[part, z + FAR, pl.ds(PAD + y, YB), :]
                    level = jnp.clip(value * down, -clip_level, clip_level)
                    if lo > y or hi < y + YB:
                        before = packed[step, part, z, pl.ds(y, YB), :].astype(F32)
                        level = jnp.where((row >= lo) & (row < hi), level, before)
                    packed[step, part, z, pl.ds(y, YB), :] = level.astype(BF16)

    stores = []

    def store_payload(step, index, rows):
        lo, hi = (bound // YB * YB for bound in rows)
        if lo < hi:
            stores.append(
                pltpu.make_async_copy(
                    packed.at[step, :, :, pl.ds(lo, hi - lo)],
                    stored_hbm.at[0, step, :, :, pl.ds(lo, hi - lo)],
                    out_sem.at[1 + step * len(row_parts) + index],
                )
            )
            stores[-1].start()

    for index in range(1, len(row_parts) + 1):
        pass_on(index)

    last = len(row_parts) - 1
    done = [0, 0, 0, 0]
    for index, (lo, hi) in enumerate(row_parts):
        @pl.when(has_down)
        def _():
            for copy in (forward_up(0) if index == 0 else []) + forward_up(index + 1):
                copy.wait_recv()

        @pl.when(has_up)
        def _():
            for copy in (forward_down(0) if index == 0 else []) + forward_down(index + 1):
                copy.wait_recv()

        widen((lo, hi))
        compress(0, (lo, hi))
        store_payload(0, index, (lo, hi))
        ends = [ROWS if index == last else hi - 2 * (k + 1) for k in range(4)]
        wide_group = GROUP * (1 if hi - lo > 32 else 2)
        span = [(first, end) for first, end in zip(done, ends)]
        theirs.rows(span[0])
        over(17, lambda i: i - 4, wide_group, theirs.velocity)
        theirs.rows(span[1])
        image = image_of(1 - peer, 1)
        over(14, lambda i: i - 3, wide_group, lambda zs: theirs.stress(zs, image))
        compress(1, span[1])
        store_payload(1, index, span[1])
        theirs.rows(span[2])
        over(11, lambda i: i - 1, wide_group, theirs.velocity)
        theirs.rows(span[3])
        image = image_of(1 - peer, 2)
        over(DEPTH, lambda i: i, wide_group, lambda zs: theirs.stress(zs, image))
        compress(2, span[3])
        store_payload(2, index, span[3])
        done = ends

    for index in range(across_count):
        across(index).wait_send()

    @pl.when(has_up)
    def _():
        for copy in mat_up():
            copy.wait_send()
        for step in range(STEPS):
            for copy in halo_up(step):
                copy.wait_send()

    @pl.when(has_down)
    def _():
        for copy in mat_down():
            copy.wait_send()
        for step in range(STEPS):
            for copy in halo_down(step):
                copy.wait_send()

    for index in range(len(row_parts) + 1):
        each(passes_up, lambda: forward_up(index), sent)
        each(passes_down, lambda: forward_down(index), sent)
        each(below_cross, lambda: straight_up(index), sent)
        each(above_cross, lambda: straight_down(index), sent)

    store_final.wait()
    for copy in stores:
        copy.wait()


def per_device(slabs, wavefield, buoyancy, lame_lambda, shear_modulus, scale_exponents, source_cells, wavelet):
    hbm = pl.BlockSpec(memory_space=pl.ANY)
    vmem = pl.BlockSpec(memory_space=pltpu.VMEM)
    smem = pl.BlockSpec(memory_space=pltpu.SMEM)
    parts = len(ROW_CUTS) - 1
    dma = pltpu.SemaphoreType.DMA
    final, stored, statistics = pl.pallas_call(
        functools.partial(kernel, slabs),
        out_shape=(
            jax.ShapeDtypeStruct(wavefield.shape, F32),
            jax.ShapeDtypeStruct((1, STEPS, 9, DEPTH, ROWS, COLS), BF16),
            jax.ShapeDtypeStruct((2, STEPS), F32),
        ),
        in_specs=[hbm, hbm, hbm, hbm, vmem, smem, smem],
        out_specs=(hbm, hbm, vmem),
        scratch_shapes=[
            pltpu.VMEM((9, DEPTH + 2 * OWN, ROWS + 2 * PAD, COLS), F32),
            pltpu.VMEM((9, DEPTH + 2 * FAR, ROWS + 2 * PAD, COLS), F32),
            pltpu.VMEM((STEPS + 1, 9, DEPTH, ROWS, COLS), BF16),
            pltpu.VMEM((STEPS, 6, 2, ROWS, COLS), BF16),
            pltpu.VMEM((STEPS, 3, 3, ROWS, COLS), BF16),
            pltpu.VMEM((STEPS, 6, 2, ROWS, COLS), BF16),
            pltpu.VMEM((STEPS, 3, 3, ROWS, COLS), BF16),
            pltpu.VMEM((DEPTH + 2 * BUO, ROWS, COLS), F32),
            pltpu.VMEM((DEPTH + 2 * MOD, ROWS, COLS), F32),
            pltpu.VMEM((DEPTH + 2 * MOD, ROWS, COLS), F32),
            pltpu.VMEM((9, DEPTH + 2 * FAR, ROWS, COLS), BF16),
            pltpu.VMEM((STEPS, 9, DEPTH, ROWS, COLS), BF16),
            pltpu.VMEM((9 * ROWS, COLS), F32),
            pltpu.VMEM((9 * ROWS, COLS), F32),
            pltpu.VMEM((9 * ROWS // BLOCK, COLS), F32),
            pltpu.VMEM((STEPS, 3, YB, COLS), F32),
            pltpu.VMEM((2, 8, COLS), F32),
            pltpu.VMEM((2, max(LOW, slabs // LOW), 8, COLS), F32),
            dma((12,)),
            dma((1 + STEPS * parts,)),
            dma((STEPS, 2, 2)),
            dma((STEPS, 2, 2)),
            dma((3, 2)),
            dma((3, 2)),
            dma((1 + 2 * parts,)),
            dma((1 + 2 * parts,)),
            dma((1 + parts, 2, 2)),
            dma((1 + parts, 2, 2)),
            dma((2, max(LOW, slabs // LOW))),
            dma((2, max(LOW, slabs // LOW))),
        ]
        + ([pltpu.VMEM((2, 2 * COLS, COLS), BF16)] if MATMUL_X else []),
        compiler_params=pltpu.CompilerParams(
            collective_id=0, has_side_effects=True, vmem_limit_bytes=60 * 1024 * 1024
        ),
        name="elastic_steps",
    )(
        wavefield, buoyancy, lame_lambda, shear_modulus,
        scale_exponents.reshape(9 * ROWS // BLOCK, COLS // BLOCK), source_cells,
        wavelet.transpose(1, 0, 2),
    )
    return final, stored, statistics.T[None]


def solution(mesh):
    return jax.shard_map(
        functools.partial(per_device, mesh.shape["space"]),
        mesh=mesh,
        in_specs=(
            P("peer", None, "space", None, None),
            P("space", None, None),
            P("space", None, None),
            P("space", None, None),
            P(None, "space", None, None),
            P(),
            P(),
        ),
        out_specs=(
            P("peer", None, "space", None, None),
            P("peer", None, None, "space", None, None),
            P("peer", None, None),
        ),
        check_vma=False,
    )
```

time: 143 us -> 85.4 us (0.60)
  the two profiles are of different devices: /device:TPU:2 before, /device:TPU:1 now
where the time goes in v2:
time: 85.4 us; the launch traced here: 85.2 us
  Pallas kernels  78.7 us (92%)
  local copies, waits for them, and re-layouts  5.87 us (7%)
    pallas_call x1, Pallas kernels, per_device(): pl.pallas_call(functools.partial(kernel, slabs), out_shape=(jax.ShapeDtyp...  78.7 us
    unnamed x7, local copies, waits for them, and re-layouts  5.87 us

profile of v2, /device:TPU:1, one launch (start us, length us, event | category | flops | bytes accessed | tf_op | source)
XLA Modules:
  0.0 85.2 jit_solution(15286738068293814704)
XLA Ops:
  0.6 78.7 %elastic_steps.1 = (f32[1,9,8,64,128]{4,3,2,1,0:T(8,128)}, bf16[1,3,9,8,64,128]{5,4,3,2,1,0:T(8,128)(2,1)}, f32[2,3]{1,0:T(2,128)}) custom-call(f32[1,9,8,64,128]{4,3,2,1,0:T(8,128)} %wave_hbm.1, f32[8,64,128]{2,1,0:T(8,128)} %buo_hbm.1, f32[8,64,128]{2,1,0:T(8,128)} %lame_hbm.1, f32[8,64,128]{2,1,0:T(8,128)} %shear_hbm.1, s32[72,16]{1,0:T(8,128)} %bitcast.5, ...), custom_call_target="tpu_custom_call" | custom-call | tf_op jit(solution)/shard_map/elastic_steps/pallas_call | solution.py:698
  79.4 0.0 copy-start
  79.4 3.5 %copy.13 = f32[1,9,8,64,128]{4,3,2,1,0:T(8,128)} copy(f32[1,9,8,64,128]{4,3,2,1,0:T(8,128)} %get-tuple-element.12) | data formatting | bytes 4718592
  82.9 0.0 copy-done
  82.9 0.0 copy-start.1
  82.9 1.8 %copy.14 = bf16[1,3,9,8,64,128]{5,4,3,2,1,0:T(8,128)(2,1)} copy(bf16[1,3,9,8,64,128]{5,4,3,2,1,0:T(8,128)(2,1)S(1)} %copy-done) | data formatting | bytes 7077888
  84.7 0.0 copy-done.1
  84.7 0.6 copy.15
Async XLA Ops:
  79.4 3.5 %copy-start = (bf16[1,3,9,8,64,128]{5,4,3,2,1,0:T(8,128)(2,1)S(1)}, bf16[1,3,9,8,64,128]{5,4,3,2,1,0:T(8,128)(2,1)}, u32[]{:S(2)}) copy-start(bf16[1,3,9,8,64,128]{5,4,3,2,1,0:T(8,128)(2,1)} %get-tuple-element.13) | copy-start | bytes 10616836
  82.9 1.8 %copy-start.1 = (f32[2,3]{1,0:T(2,128)S(1)}, f32[2,3]{1,0:T(2,128)}, u32[]{:S(2)}) copy-start(f32[2,3]{1,0:T(2,128)} %get-tuple-element.8) | copy-start | bytes 76

commit v3 on v2

--- a/solution.py
+++ b/solution.py
@@ -87,8 +87,7 @@
         return 27.0 * (f - before) - (after - far)
 
     def dy(self, part, z, forward):
-        window = self.ref[part, z + self.lead, pl.ds(self.y, self.n + 2 * PAD), :]
-        get = lambda shift: window[PAD + shift : PAD + shift + self.n]
+        get = lambda shift: self.ref[part, z + self.lead, pl.ds(self.y + PAD + shift, self.n), :]
         if forward:
             return get(1) - get(0), get(2) - get(-1)
         return get(0) - get(-1), get(1) - get(-2)
@@ -158,8 +157,8 @@
     slabs,
     wave_hbm, buo_hbm, lame_hbm, shear_hbm, exps, cells, wavelet,
     final_hbm, stored_hbm, stats_out,
-    own, other, mirror, low_a, low_b, high_a, high_b, buo, lame, shear, got, packed,
-    up_rows, down_rows, exp_rows, sums, stat_src, stat_rx,
+    own, other, mirror, low_a, low_b, high_a, high_b, buo, lame, shear, mat_out, mat_in, got, packed,
+    up_rows, down_rows, exp_rows, sums, stat_src, stat_rx, image_own, image_far,
     in_sem, out_sem, halo_send, halo_recv, mat_send, mat_recv,
     x_send, x_recv, fwd_send, fwd_recv, stat_send, stat_recv, *extra,
 ):
@@ -245,8 +244,6 @@
     def _():
         clear(1, FAR + DEPTH)
 
-    sums[...] = jnp.zeros_like(sums)
-
     for copy in loads:
         copy.wait()
 
@@ -255,13 +252,37 @@
         for z in (0, 1, 2, 5, 6, 7):
             mirror[0, part, z] = own[part, z + OWN, inner, :].astype(BF16)
 
+    mat_layers = ((0, buo, BUO), (BUO, lame, MOD), (BUO + MOD, shear, MOD))
+    for copy in mat_loads:
+        copy.wait()
+    for at, target, lead in mat_layers:
+        for z in range(lead):
+            mat_out[0, at + z] = target[DEPTH + z].astype(BF16)
+            mat_out[1, at + z] = target[lead + z].astype(BF16)
+
+    def place_sources(target, first_z, count, shot, step):
+        place = lax.broadcasted_iota(jnp.int32, (ROWS, COLS), 0) * COLS + lanes((ROWS, COLS))
+
+        @pl.loop(0, count)
+        def _(i):
+            first = (me * DEPTH + first_z + i) * ROWS * COLS
+            total = jnp.zeros((ROWS, COLS), F32)
+            for j in range(SOURCES):
+                total = total + jnp.where(place == cells[shot, j] - first, wavelet[step, shot, j], 0.0)
+            target[i] = total
+
+    for step in range(STEPS):
+        place_sources(image_own.at[step], 0, DEPTH, peer, step)
+
     greeted = [flag.astype(jnp.int32) for flag in (has_up, has_down, below_cross, above_cross)]
     pl.semaphore_wait(barrier, 1 + len(near_peers) + len(wide_peers) + sum(greeted))
 
     def halo_up(step):
         return [
-            remote(mirror.at[step, pl.ds(0, 6), pl.ds(6, 2)], low_a.at[step],
+            remote(mirror.at[step, pl.ds(0, 6), pl.ds(7, 1)], low_a.at[step, :, pl.ds(1, 1)],
                    halo_send.at[step, 0, 0], halo_recv.at[step, 0, 0], up),
+            remote(mirror.at[step, pl.ds(VZ, 1), pl.ds(6, 1)], low_a.at[step, pl.ds(VZ, 1), pl.ds(0, 1)],
+                   halo_send.at[step, 0, 2], halo_recv.at[step, 0, 2], up),
             remote(mirror.at[step, pl.ds(6, 3), pl.ds(5, 3)], low_b.at[step],
                    halo_send.at[step, 0, 1], halo_recv.at[step, 0, 1], up),
         ]
@@ -274,19 +295,31 @@
                    halo_send.at[step, 1, 1], halo_recv.at[step, 1, 1], down),
         ]
 
-    def mat_up():
-        return [
-            remote(target.at[pl.ds(DEPTH, lead)], target.at[pl.ds(0, lead)],
-                   mat_send.at[k, 0], mat_recv.at[k, 0], up)
-            for k, (_, target, lead) in enumerate(tables)
-        ]
-
-    def mat_down():
-        return [
-            remote(target.at[pl.ds(lead, lead)], target.at[pl.ds(lead + DEPTH, lead)],
-                   mat_send.at[k, 1], mat_recv.at[k, 1], down)
-            for k, (_, target, lead) in enumerate(tables)
-        ]
+    def mat_copy(kind, side, device):
+        layers = pl.ds(0, BUO) if kind == 0 else pl.ds(BUO, 2 * MOD)
+        return remote(mat_out.at[side, layers], mat_in.at[side, layers],
+                      mat_send.at[kind, side], mat_recv.at[kind, side], device)
+
+    def each(flag, copies, act):
+        @pl.when(flag)
+        def _():
+            for copy in copies():
+                act(copy)
+
+    begin, sent = (lambda copy: copy.start()), (lambda copy: copy.wait_send())
+
+    def send_mats(kind):
+        each(has_up, lambda: [mat_copy(kind, 0, up)], begin)
+        each(has_down, lambda: [mat_copy(kind, 1, down)], begin)
+
+    def take_mats(kind):
+        for side, flag, device in ((0, has_down, up), (1, has_up, down)):
+            @pl.when(flag)
+            def _(side=side, device=device):
+                mat_copy(kind, side, device).wait_recv()
+                for at, target, lead in mat_layers[:1] if kind == 0 else mat_layers[1:]:
+                    for z in range(lead):
+                        target[z + (lead + DEPTH if side else 0)] = mat_in[side, at + z].astype(F32)
 
     def send_halos(step):
         @pl.when(has_up)
@@ -299,45 +332,8 @@
             for copy in halo_down(step):
                 copy.start()
 
+    send_mats(0)
     send_halos(0)
-    for copy in mat_loads:
-        copy.wait()
-
-    @pl.when(has_up)
-    def _():
-        for copy in mat_up():
-            copy.start()
-
-    @pl.when(has_down)
-    def _():
-        for copy in mat_down():
-            copy.start()
-
-    spread = (
-        lax.broadcasted_iota(jnp.int32, (COLS // BLOCK, COLS), 0)
-        == lanes((COLS // BLOCK, COLS)) // BLOCK
-    ).astype(F32)
-    exp_rows[...] = jnp.dot(
-        exps[...].astype(F32), spread, preferred_element_type=F32, precision=lax.Precision.HIGHEST
-    )
-
-    @pl.loop(0, 9 * ROWS // BLOCK)
-    def _(i):
-        level = jnp.broadcast_to(exp_rows[pl.ds(i, 1), :], (BLOCK, COLS))
-        upscale = jnp.ones((BLOCK, COLS), F32)
-        downscale = upscale
-        for exponent in (-2, -1, 1, 2):
-            chosen = jnp.abs(level - exponent) < 0.5
-            upscale = jnp.where(chosen, 2.0**exponent, upscale)
-            downscale = jnp.where(chosen, 2.0**-exponent, downscale)
-        up_rows[pl.ds(pl.multiple_of(i * BLOCK, BLOCK), BLOCK), :] = upscale
-        down_rows[pl.ds(pl.multiple_of(i * BLOCK, BLOCK), BLOCK), :] = downscale
-
-    @pl.loop(0, 9)
-    def _(part):
-        for z in range(DEPTH + 2 * FAR):
-            other[part, z, pl.ds(0, PAD), :] = zero
-            other[part, z, pl.ds(PAD + ROWS, PAD), :] = zero
 
     band = extra[0] if MATMUL_X else None
     if MATMUL_X:
@@ -397,13 +393,7 @@
     def straight_down(index):
         return forward(index, mirror.at[1], 0, False, cross_down)
 
-    def each(flag, copies, act):
-        @pl.when(flag)
-        def _():
-            for copy in copies():
-                act(copy)
-
-    begin, sent = (lambda copy: copy.start()), (lambda copy: copy.wait_send())
+    held = (me == half - 2) | (me == half + 1)
     passes_up = has_up & jnp.logical_not(below_cross)
     passes_down = has_down & jnp.logical_not(above_cross)
 
@@ -425,31 +415,58 @@
         each(below_cross, lambda: straight_up(index), begin)
         each(above_cross, lambda: straight_down(index), begin)
 
-    def image_of(shot, step):
-        def image(z, y, n):
-            first = ((me * DEPTH + z) * ROWS + y) * COLS
-            place = lax.broadcasted_iota(jnp.int32, (n, COLS), 0) * COLS + lanes((n, COLS))
-            total = jnp.zeros((n, COLS), F32)
-            for j in range(SOURCES):
-                total = total + jnp.where(place == cells[shot, j] - first, wavelet[step, shot, j], 0.0)
-            return total
-
-        return image
+    def send_rest():
+        for index in range(2, len(row_parts) + 1):
+            send_across(index)
+
+    def prepare():
+        spread = (
+            lax.broadcasted_iota(jnp.int32, (COLS // BLOCK, COLS), 0)
+            == lanes((COLS // BLOCK, COLS)) // BLOCK
+        ).astype(F32)
+        exp_rows[...] = jnp.dot(
+            exps[...].astype(F32), spread, preferred_element_type=F32, precision=lax.Precision.HIGHEST
+        )
+
+        @pl.loop(0, 9 * ROWS // BLOCK)
+        def _(i):
+            level = jnp.broadcast_to(exp_rows[pl.ds(i, 1), :], (BLOCK, COLS))
+            upscale = jnp.ones((BLOCK, COLS), F32)
+            downscale = upscale
+            for exponent in (-2, -1, 1, 2):
+                chosen = jnp.abs(level - exponent) < 0.5
+                upscale = jnp.where(chosen, 2.0**exponent, upscale)
+                downscale = jnp.where(chosen, 2.0**-exponent, downscale)
+            up_rows[pl.ds(pl.multiple_of(i * BLOCK, BLOCK), BLOCK), :] = upscale
+            down_rows[pl.ds(pl.multiple_of(i * BLOCK, BLOCK), BLOCK), :] = downscale
+
+        @pl.loop(0, 9)
+        def _(part):
+            for z in range(DEPTH + 2 * FAR):
+                other[part, z, pl.ds(0, PAD), :] = zero
+                other[part, z, pl.ds(PAD + ROWS, PAD), :] = zero
+        place_sources(image_far.at[pl.ds(0, DEPTH + 2 * MOD)], -MOD, DEPTH + 2 * MOD, 1 - peer, 1)
+        place_sources(image_far.at[pl.ds(DEPTH + 2 * MOD, DEPTH)], 0, DEPTH, 1 - peer, 2)
 
     mine = Slab(own, OWN, buo, lame, shear, band).rows((0, ROWS))
 
-    def record(step, count, place):
+    def copy_rounded(step, zs):
+        @pl.loop(0, 9)
+        def _(part):
+            for z in zs:
+                mirror[step + 1, part, z] = mine.at(part, z).astype(BF16)
+
+    def tally(step):
         def body(k, carry):
-            part = k // (count // 2)
-            down = down_rows[pl.ds(pl.multiple_of(part * ROWS, ROWS), ROWS), :]
+            part = k // (DEPTH // 2)
+            down_scale = down_rows[pl.ds(pl.multiple_of(part * ROWS, ROWS), ROWS), :]
             up_scale = up_rows[pl.ds(pl.multiple_of(part * ROWS, ROWS), ROWS), :]
             sizes, misfits, squares = carry
-            for half in range(2):
-                z = place(lax.rem(k, count // 2) * 2 + half)
+            for side in range(2):
+                z = lax.rem(k, DEPTH // 2) * 2 + side
                 value = mine.at(part, z)
-                rounded = value.astype(BF16)
-                mirror[step + 1, part, z] = rounded
-                level = jnp.clip(rounded.astype(F32) * down, -clip_level, clip_level)
+                rounded = mirror[step + 1, part, z].astype(F32)
+                level = jnp.clip(rounded * down_scale, -clip_level, clip_level)
                 misfit = value - level * up_scale
                 for y in range(0, ROWS, YB):
                     at = slice(y, y + YB)
@@ -458,121 +475,11 @@
                     squares = squares + value[at] * value[at]
             return sizes, misfits, squares
 
-        start = tuple(sums[step, k] for k in range(3))
-        for k, total in enumerate(lax.fori_loop(0, 9 * (count // 2), body, start)):
+        zeros = jnp.zeros((YB, COLS), F32)
+        for k, total in enumerate(lax.fori_loop(0, 9 * (DEPTH // 2), body, (zeros,) * 3)):
             sums[step, k] = total
 
     edges = lambda first, gap: (lambda i: first + i + (i // 3) * gap)
-
-    @pl.loop(0, STEPS)
-    def _(step):
-        @pl.when(step == 2)
-        def _():
-            pass_on(0)
-
-        image = image_of(peer, step)
-        over(5, lambda i: i + 2, GROUP, mine.velocity)
-        middle = (2, lambda i: i + 3)
-        over(*middle, GROUP, lambda zs: mine.stress(zs, image))
-        record(step, *middle)
-
-        @pl.when(step == 0)
-        def _():
-            send_across(0)
-
-        @pl.when(has_down)
-        def _():
-            for copy in halo_up(step):
-                copy.wait_recv()
-
-            @pl.when(step == 0)
-            def _():
-                for copy in mat_up():
-                    copy.wait_recv()
-
-            @pl.loop(0, 6)
-            def _(part):
-                for z in range(2):
-                    own[part, OWN - 2 + z, inner, :] = low_a[step, part, z].astype(F32)
-
-            @pl.loop(0, 3)
-            def _(part):
-                for z in range(3):
-                    own[part + 6, OWN - 3 + z, inner, :] = low_b[step, part, z].astype(F32)
-
-        @pl.when(has_up)
-        def _():
-            for copy in halo_down(step):
-                copy.wait_recv()
-
-            @pl.when(step == 0)
-            def _():
-                for copy in mat_down():
-                    copy.wait_recv()
-
-            @pl.loop(0, 6)
-            def _(part):
-                for z in range(2):
-                    own[part, OWN + DEPTH + z, inner, :] = high_a[step, part, z].astype(F32)
-
-            @pl.loop(0, 3)
-            def _(part):
-                for z in range(3):
-                    own[part + 6, OWN + DEPTH + z, inner, :] = high_b[step, part, z].astype(F32)
-
-        over(6, edges(-1, 5), GROUP, mine.velocity)
-        outer = (6, edges(0, 2))
-        over(*outer, GROUP, lambda zs: mine.stress(zs, image))
-        record(step, *outer)
-
-        @pl.when(step < STEPS - 1)
-        def _():
-            send_halos(step + 1)
-
-        @pl.when(step == 0)
-        def _():
-            send_across(1)
-
-        @pl.when(step == 1)
-        def _():
-            for index in range(2, len(row_parts) + 1):
-                send_across(index)
-
-    store_final = pltpu.make_async_copy(
-        own.at[:, pl.ds(OWN, DEPTH), inner, :], final_hbm.at[0], out_sem.at[0]
-    )
-    store_final.start()
-
-    row8 = lax.broadcasted_iota(jnp.int32, (8, COLS), 0)
-    lane8 = lanes((8, COLS))
-    tile = jnp.zeros((8, COLS), F32)
-    for step in range(STEPS):
-        for k in range(3):
-            tile = tile + jnp.where((row8 == k) & (lane8 == step), jnp.sum(sums[step, k]), 0.0)
-
-    def gather(phase, peers, mine_at, size, tile):
-        stat_src[phase] = tile
-        copies = [
-            remote(stat_src.at[phase], stat_rx.at[phase, mine_at],
-                   stat_send.at[phase, k], stat_recv.at[phase, k], device)
-            for k, device in enumerate(peers)
-        ]
-        for copy in copies:
-            copy.start()
-        stat_rx[phase, mine_at] = tile
-        for copy in copies:
-            copy.wait()
-        total = stat_rx[phase, 0]
-        for k in range(1, size):
-            total = total + stat_rx[phase, k]
-        return total
-
-    tile = gather(0, near_peers, lane_of, LOW, tile)
-    tile = gather(1, wide_peers, block, groups, tile)
-    scaled = tile * (1.0 / (9 * slabs * DEPTH * ROWS * COLS))
-    ratio = scaled[1:2] / (scaled[2:3] + energy_floor)
-    stats_out[0:1, :] = scaled[0:1, :STEPS]
-    stats_out[1:2, :] = jnp.sqrt(ratio)[:, :STEPS]
 
     theirs = Slab(other, FAR, buo, lame, shear, band)
 
@@ -607,26 +514,32 @@
                         level = jnp.where((row >= lo) & (row < hi), level, before)
                     packed[step, part, z, pl.ds(y, YB), :] = level.astype(BF16)
 
-    stores = []
+    def payload_copy(step, index, rows):
+        lo, hi = (bound // YB * YB for bound in rows)
+        if lo == hi:
+            return []
+        return [
+            pltpu.make_async_copy(
+                packed.at[step, :, :, pl.ds(lo, hi - lo)],
+                stored_hbm.at[0, step, :, :, pl.ds(lo, hi - lo)],
+                out_sem.at[1 + step * len(row_parts) + index],
+            )
+        ]
 
     def store_payload(step, index, rows):
-        lo, hi = (bound // YB * YB for bound in rows)
-        if lo < hi:
-            stores.append(
-                pltpu.make_async_copy(
-                    packed.at[step, :, :, pl.ds(lo, hi - lo)],
-                    stored_hbm.at[0, step, :, :, pl.ds(lo, hi - lo)],
-                    out_sem.at[1 + step * len(row_parts) + index],
-                )
-            )
-            stores[-1].start()
-
-    for index in range(1, len(row_parts) + 1):
-        pass_on(index)
+        for copy in payload_copy(step, index, rows):
+            copy.start()
 
     last = len(row_parts) - 1
-    done = [0, 0, 0, 0]
-    for index, (lo, hi) in enumerate(row_parts):
+
+    def ends_of(index):
+        if index < 0:
+            return [0] * 4
+        return [ROWS if index == last else row_parts[index][1] - 2 * (k + 1) for k in range(4)]
+
+    def recompute(index):
+        lo, hi = row_parts[index]
+
         @pl.when(has_down)
         def _():
             for copy in (forward_up(0) if index == 0 else []) + forward_up(index + 1):
@@ -637,43 +550,170 @@
             for copy in (forward_down(0) if index == 0 else []) + forward_down(index + 1):
                 copy.wait_recv()
 
+        if index == 0:
+            take_mats(1)
         widen((lo, hi))
         compress(0, (lo, hi))
         store_payload(0, index, (lo, hi))
-        ends = [ROWS if index == last else hi - 2 * (k + 1) for k in range(4)]
+        span = list(zip(ends_of(index - 1), ends_of(index)))
         wide_group = GROUP * (1 if hi - lo > 32 else 2)
-        span = [(first, end) for first, end in zip(done, ends)]
         theirs.rows(span[0])
         over(17, lambda i: i - 4, wide_group, theirs.velocity)
         theirs.rows(span[1])
-        image = image_of(1 - peer, 1)
+        image = lambda z, y, n: image_far[z + MOD, pl.ds(y, n), :]
         over(14, lambda i: i - 3, wide_group, lambda zs: theirs.stress(zs, image))
         compress(1, span[1])
         store_payload(1, index, span[1])
         theirs.rows(span[2])
         over(11, lambda i: i - 1, wide_group, theirs.velocity)
         theirs.rows(span[3])
-        image = image_of(1 - peer, 2)
+        image = lambda z, y, n: image_far[z + DEPTH + 2 * MOD, pl.ds(y, n), :]
         over(DEPTH, lambda i: i, wide_group, lambda zs: theirs.stress(zs, image))
         compress(2, span[3])
         store_payload(2, index, span[3])
-        done = ends
+
+    @pl.loop(0, STEPS)
+    def _(step):
+        @pl.when(step == 2)
+        def _():
+            pass_on(0)
+
+        def image(z, y, n):
+            return image_own[step, z, pl.ds(y, n), :]
+
+        over(5, lambda i: i + 2, GROUP, mine.velocity)
+        middle = (2, lambda i: i + 3)
+        over(*middle, GROUP, lambda zs: mine.stress(zs, image))
+        copy_rounded(step, (3, 4))
+
+        @pl.when(step == 0)
+        def _():
+            send_across(0)
+            prepare()
+            take_mats(0)
+
+        @pl.when(step == 2)
+        def _():
+            pass_on(1)
+
+        @pl.when(has_down)
+        def _():
+            for copy in halo_up(step):
+                copy.wait_recv()
+
+            @pl.loop(0, 6)
+            def _(part):
+                own[part, OWN - 1, inner, :] = low_a[step, part, 1].astype(F32)
+
+            own[VZ, OWN - 2, inner, :] = low_a[step, VZ, 0].astype(F32)
+
+            @pl.loop(0, 3)
+            def _(part):
+                for z in range(3):
+                    own[part + 6, OWN - 3 + z, inner, :] = low_b[step, part, z].astype(F32)
+
+        @pl.when(has_up)
+        def _():
+            for copy in halo_down(step):
+                copy.wait_recv()
+
+            @pl.loop(0, 6)
+            def _(part):
+                for z in range(2):
+                    own[part, OWN + DEPTH + z, inner, :] = high_a[step, part, z].astype(F32)
+
+            @pl.loop(0, 3)
+            def _(part):
+                for z in range(3):
+                    own[part + 6, OWN + DEPTH + z, inner, :] = high_b[step, part, z].astype(F32)
+
+        @pl.when((step == 2) & held)
+        def _():
+            send_rest()
+
+        over(6, edges(-1, 5), GROUP, mine.velocity)
+        outer = (6, edges(0, 2))
+        over(*outer, GROUP, lambda zs: mine.stress(zs, image))
+        copy_rounded(step, (0, 1, 2, 5, 6, 7))
+
+        @pl.when(step < STEPS - 1)
+        def _():
+            send_halos(step + 1)
+
+        @pl.when(step == 0)
+        def _():
+            send_mats(1)
+            send_across(1)
+
+        @pl.when((step == 1) & jnp.logical_not(held))
+        def _():
+            send_rest()
+
+        tally(step)
+
+    store_final = pltpu.make_async_copy(
+        own.at[:, pl.ds(OWN, DEPTH), inner, :], final_hbm.at[0], out_sem.at[0]
+    )
+    store_final.start()
+
+    row8 = lax.broadcasted_iota(jnp.int32, (8, COLS), 0)
+    lane8 = lanes((8, COLS))
+    tile = jnp.zeros((8, COLS), F32)
+    for step in range(STEPS):
+        for k in range(3):
+            tile = tile + jnp.where((row8 == k) & (lane8 == step), jnp.sum(sums[step, k]), 0.0)
+
+    def spread_sums(phase, peers, mine_at, tile):
+        stat_src[phase] = tile
+        stat_rx[phase, mine_at] = tile
+        copies = [
+            remote(stat_src.at[phase], stat_rx.at[phase, mine_at],
+                   stat_send.at[phase, k], stat_recv.at[phase, k], device)
+            for k, device in enumerate(peers)
+        ]
+        for copy in copies:
+            copy.start()
+        return copies
+
+    def collect_sums(phase, copies, size):
+        for copy in copies:
+            copy.wait()
+        total = stat_rx[phase, 0]
+        for k in range(1, size):
+            total = total + stat_rx[phase, k]
+        return total
+
+    sum_copies = spread_sums(0, near_peers, lane_of, tile)
+
+    for index in range(len(row_parts)):
+        if index < last:
+            pass_on(index + 2)
+        else:
+            tile = collect_sums(0, sum_copies, LOW)
+            sum_copies = spread_sums(1, wide_peers, block, tile)
+        recompute(index)
+
+    tile = collect_sums(1, sum_copies, groups)
+    scaled = tile * (1.0 / (9 * slabs * DEPTH * ROWS * COLS))
+    ratio = scaled[1:2] / (scaled[2:3] + energy_floor)
+    stats_out[0:1, :] = scaled[0:1, :STEPS]
+    stats_out[1:2, :] = jnp.sqrt(ratio)[:, :STEPS]
 
     for index in range(across_count):
         across(index).wait_send()
 
     @pl.when(has_up)
     def _():
-        for copy in mat_up():
-            copy.wait_send()
+        for kind in range(2):
+            mat_copy(kind, 0, up).wait_send()
         for step in range(STEPS):
             for copy in halo_up(step):
                 copy.wait_send()
 
     @pl.when(has_down)
     def _():
-        for copy in mat_down():
-            copy.wait_send()
+        for kind in range(2):
+            mat_copy(kind, 1, down).wait_send()
         for step in range(STEPS):
             for copy in halo_down(step):
                 copy.wait_send()
@@ -685,8 +725,11 @@
         each(above_cross, lambda: straight_down(index), sent)
 
     store_final.wait()
-    for copy in stores:
-        copy.wait()
+    for index, part_rows in enumerate(row_parts):
+        span = list(zip(ends_of(index - 1), ends_of(index)))
+        for step, rows in enumerate((part_rows, span[1], span[3])):
+            for copy in payload_copy(step, index, rows):
+                copy.wait()
 
 
 def per_device(slabs, wavefield, buoyancy, lame_lambda, shear_modulus, scale_exponents, source_cells, wavelet):
@@ -715,6 +758,8 @@
             pltpu.VMEM((DEPTH + 2 * BUO, ROWS, COLS), F32),
             pltpu.VMEM((DEPTH + 2 * MOD, ROWS, COLS), F32),
             pltpu.VMEM((DEPTH + 2 * MOD, ROWS, COLS), F32),
+            pltpu.VMEM((2, BUO + 2 * MOD, ROWS, COLS), BF16),
+            pltpu.VMEM((2, BUO + 2 * MOD, ROWS, COLS), BF16),
             pltpu.VMEM((9, DEPTH + 2 * FAR, ROWS, COLS), BF16),
             pltpu.VMEM((STEPS, 9, DEPTH, ROWS, COLS), BF16),
             pltpu.VMEM((9 * ROWS, COLS), F32),
@@ -723,12 +768,14 @@
             pltpu.VMEM((STEPS, 3, YB, COLS), F32),
             pltpu.VMEM((2, 8, COLS), F32),
             pltpu.VMEM((2, max(LOW, slabs // LOW), 8, COLS), F32),
+            pltpu.VMEM((STEPS, DEPTH, ROWS, COLS), F32),
+            pltpu.VMEM((2 * DEPTH + 2 * MOD, ROWS, COLS), F32),
             dma((12,)),
             dma((1 + STEPS * parts,)),
-            dma((STEPS, 2, 2)),
-            dma((STEPS, 2, 2)),
-            dma((3, 2)),
-            dma((3, 2)),
+            dma((STEPS, 2, 3)),
+            dma((STEPS, 2, 3)),
+            dma((2, 2)),
+            dma((2, 2)),
             dma((1 + 2 * parts,)),
             dma((1 + 2 * parts,)),
             dma((1 + parts, 2, 2)),

time: 85.4 us -> 64.7 us (0.76)
  the two profiles are of different devices: /device:TPU:1 before, /device:TPU:2 now
where the time goes in v3:
time: 64.7 us; the launch traced here: 64.5 us
  Pallas kernels  58 us (90%)
  local copies, waits for them, and re-layouts  5.87 us (9%)
  between operations  0.65 us (1%)
    pallas_call x1, Pallas kernels, per_device(): pl.pallas_call(functools.partial(kernel, slabs), out_shape=(jax.ShapeDtyp...  58 us
    unnamed x7, local copies, waits for them, and re-layouts  5.87 us

profile of v3, /device:TPU:2, one launch (start us, length us, event | category | flops | bytes accessed | tf_op | source)
XLA Modules:
  0.0 64.5 jit_solution(6795321664322302254)
XLA Ops:
  0.6 58.0 %elastic_steps.1 = (f32[1,9,8,64,128]{4,3,2,1,0:T(8,128)}, bf16[1,3,9,8,64,128]{5,4,3,2,1,0:T(8,128)(2,1)}, f32[2,3]{1,0:T(2,128)}) custom-call(f32[1,9,8,64,128]{4,3,2,1,0:T(8,128)} %wave_hbm.1, f32[8,64,128]{2,1,0:T(8,128)} %buo_hbm.1, f32[8,64,128]{2,1,0:T(8,128)} %lame_hbm.1, f32[8,64,128]{2,1,0:T(8,128)} %shear_hbm.1, s32[72,16]{1,0:T(8,128)} %bitcast.5, ...), custom_call_target="tpu_custom_call" | custom-call | tf_op jit(solution)/shard_map/elastic_steps/pallas_call | solution.py:741
  58.6 0.0 copy-start
  58.6 3.5 %copy.13 = f32[1,9,8,64,128]{4,3,2,1,0:T(8,128)} copy(f32[1,9,8,64,128]{4,3,2,1,0:T(8,128)} %get-tuple-element.12) | data formatting | bytes 4718592
  62.1 0.0 copy-done
  62.1 0.0 copy-start.1
  62.1 1.8 %copy.14 = bf16[1,3,9,8,64,128]{5,4,3,2,1,0:T(8,128)(2,1)} copy(bf16[1,3,9,8,64,128]{5,4,3,2,1,0:T(8,128)(2,1)S(1)} %copy-done) | data formatting | bytes 7077888
  63.9 0.0 copy-done.1
  63.9 0.6 copy.15
Async XLA Ops:
  58.6 3.5 %copy-start = (bf16[1,3,9,8,64,128]{5,4,3,2,1,0:T(8,128)(2,1)S(1)}, bf16[1,3,9,8,64,128]{5,4,3,2,1,0:T(8,128)(2,1)}, u32[]{:S(2)}) copy-start(bf16[1,3,9,8,64,128]{5,4,3,2,1,0:T(8,128)(2,1)} %get-tuple-element.13) | copy-start | bytes 10616836
  62.1 1.8 %copy-start.1 = (f32[2,3]{1,0:T(2,128)S(1)}, f32[2,3]{1,0:T(2,128)}, u32[]{:S(2)}) copy-start(f32[2,3]{1,0:T(2,128)} %get-tuple-element.8) | copy-start | bytes 76

commit v4 on v3

--- a/solution.py
+++ b/solution.py
@@ -156,10 +156,10 @@
 def kernel(
     slabs,
     wave_hbm, buo_hbm, lame_hbm, shear_hbm, exps, cells, wavelet,
-    final_hbm, stored_hbm, stats_out,
-    own, other, mirror, low_a, low_b, high_a, high_b, buo, lame, shear, mat_out, mat_in, got, packed,
+    own, packed, stats_out,
+    other, mirror, low_a, low_b, high_a, high_b, buo, lame, shear, mat_out, mat_in, got,
     up_rows, down_rows, exp_rows, sums, stat_src, stat_rx, image_own, image_far,
-    in_sem, out_sem, halo_send, halo_recv, mat_send, mat_recv,
+    in_sem, halo_send, halo_recv, mat_send, mat_recv,
     x_send, x_recv, fwd_send, fwd_recv, stat_send, stat_recv, *extra,
 ):
     me, peer = lax.axis_index("space"), lax.axis_index("peer")
@@ -514,22 +514,6 @@
                         level = jnp.where((row >= lo) & (row < hi), level, before)
                     packed[step, part, z, pl.ds(y, YB), :] = level.astype(BF16)
 
-    def payload_copy(step, index, rows):
-        lo, hi = (bound // YB * YB for bound in rows)
-        if lo == hi:
-            return []
-        return [
-            pltpu.make_async_copy(
-                packed.at[step, :, :, pl.ds(lo, hi - lo)],
-                stored_hbm.at[0, step, :, :, pl.ds(lo, hi - lo)],
-                out_sem.at[1 + step * len(row_parts) + index],
-            )
-        ]
-
-    def store_payload(step, index, rows):
-        for copy in payload_copy(step, index, rows):
-            copy.start()
-
     last = len(row_parts) - 1
 
     def ends_of(index):
@@ -554,7 +538,6 @@
             take_mats(1)
         widen((lo, hi))
         compress(0, (lo, hi))
-        store_payload(0, index, (lo, hi))
         span = list(zip(ends_of(index - 1), ends_of(index)))
         wide_group = GROUP * (1 if hi - lo > 32 else 2)
         theirs.rows(span[0])
@@ -563,14 +546,12 @@
         image = lambda z, y, n: image_far[z + MOD, pl.ds(y, n), :]
         over(14, lambda i: i - 3, wide_group, lambda zs: theirs.stress(zs, image))
         compress(1, span[1])
-        store_payload(1, index, span[1])
         theirs.rows(span[2])
         over(11, lambda i: i - 1, wide_group, theirs.velocity)
         theirs.rows(span[3])
         image = lambda z, y, n: image_far[z + DEPTH + 2 * MOD, pl.ds(y, n), :]
         over(DEPTH, lambda i: i, wide_group, lambda zs: theirs.stress(zs, image))
         compress(2, span[3])
-        store_payload(2, index, span[3])
 
     @pl.loop(0, STEPS)
     def _(step):
@@ -650,11 +631,6 @@
             send_rest()
 
         tally(step)
-
-    store_final = pltpu.make_async_copy(
-        own.at[:, pl.ds(OWN, DEPTH), inner, :], final_hbm.at[0], out_sem.at[0]
-    )
-    store_final.start()
 
     row8 = lax.broadcasted_iota(jnp.int32, (8, COLS), 0)
     lane8 = lanes((8, COLS))
@@ -724,12 +700,21 @@
         each(below_cross, lambda: straight_up(index), sent)
         each(above_cross, lambda: straight_down(index), sent)
 
-    store_final.wait()
-    for index, part_rows in enumerate(row_parts):
-        span = list(zip(ends_of(index - 1), ends_of(index)))
-        for step, rows in enumerate((part_rows, span[1], span[3])):
-            for copy in payload_copy(step, index, rows):
-                copy.wait()
+
+def write_out(own, packed, sums, final_hbm, stored_hbm, stats_out, sem):
+    copies = [
+        pltpu.make_async_copy(packed.at[step], stored_hbm.at[0, step], sem.at[step]) for step in range(STEPS)
+    ]
+    copies.append(
+        pltpu.make_async_copy(
+            own.at[:, pl.ds(OWN, DEPTH), pl.ds(PAD, ROWS), :], final_hbm.at[0], sem.at[STEPS]
+        )
+    )
+    for copy in copies:
+        copy.start()
+    stats_out[...] = sums[...]
+    for copy in copies:
+        copy.wait()
 
 
 def per_device(slabs, wavefield, buoyancy, lame_lambda, shear_modulus, scale_exponents, source_cells, wavelet):
@@ -738,17 +723,16 @@
     smem = pl.BlockSpec(memory_space=pltpu.SMEM)
     parts = len(ROW_CUTS) - 1
     dma = pltpu.SemaphoreType.DMA
-    final, stored, statistics = pl.pallas_call(
+    own, packed, statistics = pl.pallas_call(
         functools.partial(kernel, slabs),
         out_shape=(
-            jax.ShapeDtypeStruct(wavefield.shape, F32),
-            jax.ShapeDtypeStruct((1, STEPS, 9, DEPTH, ROWS, COLS), BF16),
-            jax.ShapeDtypeStruct((2, STEPS), F32),
+            pltpu.VMEM((9, DEPTH + 2 * OWN, ROWS + 2 * PAD, COLS), F32),
+            pltpu.VMEM((STEPS, 9, DEPTH, ROWS, COLS), BF16),
+            pltpu.VMEM((2, STEPS), F32),
         ),
         in_specs=[hbm, hbm, hbm, hbm, vmem, smem, smem],
-        out_specs=(hbm, hbm, vmem),
+        out_specs=(vmem, vmem, vmem),
         scratch_shapes=[
-            pltpu.VMEM((9, DEPTH + 2 * OWN, ROWS + 2 * PAD, COLS), F32),
             pltpu.VMEM((9, DEPTH + 2 * FAR, ROWS + 2 * PAD, COLS), F32),
             pltpu.VMEM((STEPS + 1, 9, DEPTH, ROWS, COLS), BF16),
             pltpu.VMEM((STEPS, 6, 2, ROWS, COLS), BF16),
@@ -761,7 +745,6 @@
             pltpu.VMEM((2, BUO + 2 * MOD, ROWS, COLS), BF16),
             pltpu.VMEM((2, BUO + 2 * MOD, ROWS, COLS), BF16),
             pltpu.VMEM((9, DEPTH + 2 * FAR, ROWS, COLS), BF16),
-            pltpu.VMEM((STEPS, 9, DEPTH, ROWS, COLS), BF16),
             pltpu.VMEM((9 * ROWS, COLS), F32),
             pltpu.VMEM((9 * ROWS, COLS), F32),
             pltpu.VMEM((9 * ROWS // BLOCK, COLS), F32),
@@ -771,7 +754,6 @@
             pltpu.VMEM((STEPS, DEPTH, ROWS, COLS), F32),
             pltpu.VMEM((2 * DEPTH + 2 * MOD, ROWS, COLS), F32),
             dma((12,)),
-            dma((1 + STEPS * parts,)),
             dma((STEPS, 2, 3)),
             dma((STEPS, 2, 3)),
             dma((2, 2)),
@@ -785,7 +767,7 @@
         ]
         + ([pltpu.VMEM((2, 2 * COLS, COLS), BF16)] if MATMUL_X else []),
         compiler_params=pltpu.CompilerParams(
-            collective_id=0, has_side_effects=True, vmem_limit_bytes=60 * 1024 * 1024
+            collective_id=0, has_side_effects=True, vmem_limit_bytes=55 * 1024 * 1024
         ),
         name="elastic_steps",
     )(
@@ -793,6 +775,19 @@
         scale_exponents.reshape(9 * ROWS // BLOCK, COLS // BLOCK), source_cells,
         wavelet.transpose(1, 0, 2),
     )
+    final, stored, statistics = pl.pallas_call(
+        write_out,
+        out_shape=(
+            jax.ShapeDtypeStruct(wavefield.shape, F32),
+            jax.ShapeDtypeStruct((1, STEPS, 9, DEPTH, ROWS, COLS), BF16),
+            jax.ShapeDtypeStruct((2, STEPS), F32),
+        ),
+        in_specs=[vmem, vmem, vmem],
+        out_specs=(hbm, hbm, vmem),
+        scratch_shapes=[dma((STEPS + 1,))],
+        compiler_params=pltpu.CompilerParams(vmem_limit_bytes=8 * 1024 * 1024),
+        name="write_out",
+    )(own, packed, statistics)
     return final, stored, statistics.T[None]
 
 

time: 64.7 us -> 60.8 us (0.940)
  local copies, waits for them, and re-layouts: 5.87 us -> 0 us
  Pallas kernels: 58 us -> 59.8 us
    unnamed x7 -> x0, local copies, waits for them, and re-layouts: 5.87 us -> none
    pallas_call x1 -> x2, Pallas kernels: 58 us -> 59.8 us  [the longest x1 56.6 us: per_device(): pl.pallas_call(functools.partial(kernel, slabs), out_shape=(pltpu.VMEM((9...]
where the time goes in v4:
time: 60.8 us; the launch traced here: 60.4 us
  Pallas kernels  59.8 us (98%)
  between operations  0.64 us (1%)
    pallas_call x1, Pallas kernels, per_device(): pl.pallas_call(functools.partial(kernel, slabs), out_shape=(pltpu.VMEM((9...  56.6 us
    pallas_call x1, Pallas kernels, per_device(): pl.pallas_call(write_out, out_shape=(jax.ShapeDtypeStruct(wavefield.shape...  3.17 us

profile of v4, /device:TPU:2, one launch (start us, length us, event | category | flops | bytes accessed | tf_op | source)
XLA Modules:
  0.0 60.4 jit_solution(16702546040142247512)
XLA Ops:
  0.6 56.6 %elastic_steps.1 = (f32[9,14,80,128]{3,2,1,0:T(8,128)S(1)}, bf16[3,9,8,64,128]{4,3,2,1,0:T(8,128)(2,1)S(1)}, f32[2,3]{1,0:T(2,128)S(1)}) custom-call(f32[1,9,8,64,128]{4,3,2,1,0:T(8,128)} %wave_hbm.1, f32[8,64,128]{2,1,0:T(8,128)} %buo_hbm.1, f32[8,64,128]{2,1,0:T(8,128)} %lame_hbm.1, f32[8,64,128]{2,1,0:T(8,128)} %shear_hbm.1, s32[72,16]{1,0:T(8,128)} %bitcast.5, ...), custom_call_target="tpu_custom_call" | custom-call | tf_op jit(solution)/shard_map/elastic_steps/pallas_call | solution.py:726
  57.3 3.2 %write_out.1 = (f32[1,9,8,64,128]{4,3,2,1,0:T(8,128)}, bf16[1,3,9,8,64,128]{5,4,3,2,1,0:T(8,128)(2,1)}, f32[2,3]{1,0:T(2,128)}) custom-call(f32[9,14,80,128]{3,2,1,0:T(8,128)S(1)} %get-tuple-element.9.own, bf16[3,9,8,64,128]{4,3,2,1,0:T(8,128)(2,1)S(1)} %get-tuple-element.10.packed, f32[2,3]{1,0:T(2,128)S(1)} %get-tuple-element.11.sums), custom_call_target="tpu_custom_call" | custom-call | tf_op jit(solution)/shard_map/write_out/pallas_call | solution.py:778

commit v5 on v4

--- a/solution.py
+++ b/solution.py
@@ -18,12 +18,14 @@
 PAD = 8
 YB = 16
 GROUP = 2
+WIDE_GROUP = 4
 MATMUL_X = False
 OWN = 3
 FAR = 6
 BUO, MOD = 5, 3
 LOW = 8
 ROW_CUTS = (0, 32, 48, 64)
+GROUPS = ((0,), (1, 2))
 VX, VY, VZ, SXX, SYY, SXY, SZZ, SXZ, SYZ = range(9)
 clip_level = 4.0
 energy_floor = 1e-06
@@ -158,9 +160,9 @@
     wave_hbm, buo_hbm, lame_hbm, shear_hbm, exps, cells, wavelet,
     own, packed, stats_out,
     other, mirror, low_a, low_b, high_a, high_b, buo, lame, shear, mat_out, mat_in, got,
-    up_rows, down_rows, exp_rows, sums, stat_src, stat_rx, image_own, image_far,
+    up_rows, down_rows, exp_rows, sums, stat_src, stat_rx, image_own, image_far, held_over,
     in_sem, halo_send, halo_recv, mat_send, mat_recv,
-    x_send, x_recv, fwd_send, fwd_recv, stat_send, stat_recv, *extra,
+    x_send, x_recv, help_send, help_recv, fwd_send, fwd_recv, stat_send, stat_recv, *extra,
 ):
     me, peer = lax.axis_index("space"), lax.axis_index("peer")
     has_down, has_up = me > 0, me < slabs - 1
@@ -169,6 +171,12 @@
     half = slabs // 2
     below_cross, above_cross = me == half - 1, me == half
     cross_up, cross_down = (me + 1, 1 - peer), (me - 1, 1 - peer)
+    detours = ((half - 2, -2), (half - 1, -LOW), (half, LOW), (half + 1, 2))
+    flag = lambda condition: condition.astype(jnp.int32)
+    hands_over = (me >= half - 2) & (me <= half + 1)
+    helper = me + sum(flag(me == slab) * offset for slab, offset in detours)
+    helped = sum(flag(me == slab + offset) * slab for slab, offset in detours)
+    helps = helped > 0
     groups = slabs // LOW
     block, lane_of = me // LOW, lax.rem(me, LOW)
     near_peers = [(block * LOW + lax.rem(lane_of + k, LOW), peer) for k in range(1, LOW)]
@@ -185,6 +193,14 @@
     @pl.when(has_down)
     def _():
         pl.semaphore_signal(barrier, inc=1, device_id=down, device_id_type=MESH)
+
+    @pl.when(hands_over)
+    def _():
+        pl.semaphore_signal(barrier, inc=1, device_id=(helper, 1 - peer), device_id_type=MESH)
+
+    @pl.when(helps)
+    def _():
+        pl.semaphore_signal(barrier, inc=1, device_id=(helped, peer), device_id_type=MESH)
 
     @pl.when(below_cross)
     def _():
@@ -244,21 +260,10 @@
     def _():
         clear(1, FAR + DEPTH)
 
-    for copy in loads:
+    for part, copy in enumerate(loads):
         copy.wait()
-
-    @pl.loop(0, 9)
-    def _(part):
-        for z in (0, 1, 2, 5, 6, 7):
+        for z in (0, 1, 6, 7) if part < 6 else (0, 1, 2, 5, 6, 7):
             mirror[0, part, z] = own[part, z + OWN, inner, :].astype(BF16)
-
-    mat_layers = ((0, buo, BUO), (BUO, lame, MOD), (BUO + MOD, shear, MOD))
-    for copy in mat_loads:
-        copy.wait()
-    for at, target, lead in mat_layers:
-        for z in range(lead):
-            mat_out[0, at + z] = target[DEPTH + z].astype(BF16)
-            mat_out[1, at + z] = target[lead + z].astype(BF16)
 
     def place_sources(target, first_z, count, shot, step):
         place = lax.broadcasted_iota(jnp.int32, (ROWS, COLS), 0) * COLS + lanes((ROWS, COLS))
@@ -271,10 +276,19 @@
                 total = total + jnp.where(place == cells[shot, j] - first, wavelet[step, shot, j], 0.0)
             target[i] = total
 
-    for step in range(STEPS):
-        place_sources(image_own.at[step], 0, DEPTH, peer, step)
-
-    greeted = [flag.astype(jnp.int32) for flag in (has_up, has_down, below_cross, above_cross)]
+    mat_layers = ((0, buo, BUO), (BUO, lame, MOD), (BUO + MOD, shear, MOD))
+
+    def round_mats(layers_of):
+        for at, target, lead in layers_of:
+            for z in range(lead):
+                mat_out[0, at + z] = target[DEPTH + z].astype(BF16)
+                mat_out[1, at + z] = target[lead + z].astype(BF16)
+
+    for copy in mat_loads:
+        copy.wait()
+    round_mats(mat_layers[:1])
+
+    greeted = [flag(yes) for yes in (has_up, has_down, below_cross, above_cross, hands_over, helps)]
     pl.semaphore_wait(barrier, 1 + len(near_peers) + len(wide_peers) + sum(greeted))
 
     def halo_up(step):
@@ -334,6 +348,7 @@
 
     send_mats(0)
     send_halos(0)
+    place_sources(image_own.at[0], 0, DEPTH, peer, 0)
 
     band = extra[0] if MATMUL_X else None
     if MATMUL_X:
@@ -393,7 +408,7 @@
     def straight_down(index):
         return forward(index, mirror.at[1], 0, False, cross_down)
 
-    held = (me == half - 2) | (me == half + 1)
+    held = (me < 2) | (me >= slabs - 2)
     passes_up = has_up & jnp.logical_not(below_cross)
     passes_down = has_down & jnp.logical_not(above_cross)
 
@@ -406,14 +421,37 @@
         each(passes_up, lambda: forward_up(index), begin)
         each(passes_down, lambda: forward_down(index), begin)
 
+    own_way = jnp.logical_not(hands_over)
+
+    def across_copies(index):
+        return [across(0)] if index == 0 else [across(2 * index - 1), across(2 * index)]
+
     def send_across(index):
-        if index == 0:
-            across(0).start()
+        if index < 2:
+            for copy in across_copies(index):
+                copy.start()
         else:
-            across(2 * index - 1).start()
-            across(2 * index).start()
+            each(own_way, lambda: across_copies(index), begin)
         each(below_cross, lambda: straight_up(index), begin)
         each(above_cross, lambda: straight_down(index), begin)
+
+    late = pl.ds(ROW_CUTS[1], ROWS - ROW_CUTS[1])
+
+    def hand_over():
+        return [
+            remote(mirror.at[1, :, pl.ds(first, 3), late], held_over.at[:, pl.ds(3 * k, 3)],
+                   help_send.at[k], help_recv.at[k], (helper, peer))
+            for k, first in enumerate((0, 5))
+        ]
+
+    def help_across():
+        return [
+            remote(held_over.at[:, pl.ds(3 * k, 3), pl.ds(lo - ROW_CUTS[1], hi - lo)],
+                   got.at[:, pl.ds(FAR + first, 3), pl.ds(lo, hi - lo)],
+                   help_send.at[2 * i + k], x_recv.at[2 * i - 1 + k], (helped, 1 - peer))
+            for i, (lo, hi) in enumerate(row_parts, 1) if i > 1
+            for k, first in enumerate((0, 5))
+        ]
 
     def send_rest():
         for index in range(2, len(row_parts) + 1):
@@ -445,6 +483,9 @@
             for z in range(DEPTH + 2 * FAR):
                 other[part, z, pl.ds(0, PAD), :] = zero
                 other[part, z, pl.ds(PAD + ROWS, PAD), :] = zero
+        round_mats(mat_layers[1:])
+        for step in (1, 2):
+            place_sources(image_own.at[step], 0, DEPTH, peer, step)
         place_sources(image_far.at[pl.ds(0, DEPTH + 2 * MOD)], -MOD, DEPTH + 2 * MOD, 1 - peer, 1)
         place_sources(image_far.at[pl.ds(DEPTH + 2 * MOD, DEPTH)], 0, DEPTH, 1 - peer, 2)
 
@@ -514,38 +555,42 @@
                         level = jnp.where((row >= lo) & (row < hi), level, before)
                     packed[step, part, z, pl.ds(y, YB), :] = level.astype(BF16)
 
-    last = len(row_parts) - 1
 
     def ends_of(index):
         if index < 0:
             return [0] * 4
-        return [ROWS if index == last else row_parts[index][1] - 2 * (k + 1) for k in range(4)]
-
-    def recompute(index):
-        lo, hi = row_parts[index]
+        end = row_parts[GROUPS[index][-1]][1]
+        return [end if end == ROWS else end - 2 * (k + 1) for k in range(4)]
+
+    def recompute(index, between):
+        lo, hi = row_parts[GROUPS[index][0]][0], row_parts[GROUPS[index][-1]][1]
+        arriving = ([0] if index == 0 else []) + [part + 1 for part in GROUPS[index]]
 
         @pl.when(has_down)
         def _():
-            for copy in (forward_up(0) if index == 0 else []) + forward_up(index + 1):
-                copy.wait_recv()
+            for part in arriving:
+                for copy in forward_up(part):
+                    copy.wait_recv()
 
         @pl.when(has_up)
         def _():
-            for copy in (forward_down(0) if index == 0 else []) + forward_down(index + 1):
-                copy.wait_recv()
+            for part in arriving:
+                for copy in forward_down(part):
+                    copy.wait_recv()
 
         if index == 0:
             take_mats(1)
         widen((lo, hi))
         compress(0, (lo, hi))
         span = list(zip(ends_of(index - 1), ends_of(index)))
-        wide_group = GROUP * (1 if hi - lo > 32 else 2)
+        wide_group = WIDE_GROUP
         theirs.rows(span[0])
         over(17, lambda i: i - 4, wide_group, theirs.velocity)
         theirs.rows(span[1])
         image = lambda z, y, n: image_far[z + MOD, pl.ds(y, n), :]
         over(14, lambda i: i - 3, wide_group, lambda zs: theirs.stress(zs, image))
         compress(1, span[1])
+        between()
         theirs.rows(span[2])
         over(11, lambda i: i - 1, wide_group, theirs.velocity)
         theirs.rows(span[3])
@@ -573,7 +618,7 @@
             prepare()
             take_mats(0)
 
-        @pl.when(step == 2)
+        @pl.when((step == 2) & own_way)
         def _():
             pass_on(1)
 
@@ -624,13 +669,24 @@
         @pl.when(step == 0)
         def _():
             send_mats(1)
-            send_across(1)
+            each(hands_over, hand_over, begin)
+            pl.when(own_way)(lambda: send_across(1))
 
         @pl.when((step == 1) & jnp.logical_not(held))
         def _():
+            pl.when(hands_over)(lambda: send_across(1))
             send_rest()
 
         tally(step)
+
+    pl.when(hands_over)(lambda: pass_on(1))
+
+    @pl.when(helps)
+    def _():
+        for copy in hand_over():
+            copy.wait_recv()
+        for copy in help_across():
+            copy.start()
 
     row8 = lax.broadcasted_iota(jnp.int32, (8, COLS), 0)
     lane8 = lanes((8, COLS))
@@ -639,44 +695,53 @@
         for k in range(3):
             tile = tile + jnp.where((row8 == k) & (lane8 == step), jnp.sum(sums[step, k]), 0.0)
 
-    def spread_sums(phase, peers, mine_at, tile):
-        stat_src[phase] = tile
-        stat_rx[phase, mine_at] = tile
-        copies = [
-            remote(stat_src.at[phase], stat_rx.at[phase, mine_at],
+    def sum_copies(phase):
+        peers, slot = ((near_peers, lane_of), (wide_peers, block))[phase]
+        return [
+            remote(stat_src.at[phase], stat_rx.at[phase, slot],
                    stat_send.at[phase, k], stat_recv.at[phase, k], device)
             for k, device in enumerate(peers)
         ]
-        for copy in copies:
+
+    def spread_sums(phase, tile):
+        stat_src[phase] = tile
+        stat_rx[phase, (lane_of, block)[phase]] = tile
+        for copy in sum_copies(phase):
             copy.start()
-        return copies
-
-    def collect_sums(phase, copies, size):
-        for copy in copies:
+
+    def collect_sums(phase):
+        for copy in sum_copies(phase):
             copy.wait()
         total = stat_rx[phase, 0]
-        for k in range(1, size):
+        for k in range(1, (LOW, groups)[phase]):
             total = total + stat_rx[phase, k]
         return total
 
-    sum_copies = spread_sums(0, near_peers, lane_of, tile)
-
-    for index in range(len(row_parts)):
-        if index < last:
-            pass_on(index + 2)
-        else:
-            tile = collect_sums(0, sum_copies, LOW)
-            sum_copies = spread_sums(1, wide_peers, block, tile)
-        recompute(index)
-
-    tile = collect_sums(1, sum_copies, groups)
+    spread_sums(0, tile)
+    late_sums = below_cross | above_cross
+
+    def second_phase():
+        spread_sums(1, collect_sums(0))
+
+    pass_on(2)
+    pl.when(late_sums)(second_phase)
+    recompute(0, lambda: pass_on(3))
+    pl.when(jnp.logical_not(late_sums))(second_phase)
+    recompute(1, lambda: None)
+
+    tile = collect_sums(1)
     scaled = tile * (1.0 / (9 * slabs * DEPTH * ROWS * COLS))
     ratio = scaled[1:2] / (scaled[2:3] + energy_floor)
     stats_out[0:1, :] = scaled[0:1, :STEPS]
     stats_out[1:2, :] = jnp.sqrt(ratio)[:, :STEPS]
 
-    for index in range(across_count):
-        across(index).wait_send()
+    for index in range(2):
+        for copy in across_copies(index):
+            copy.wait_send()
+    for index in range(2, len(row_parts) + 1):
+        each(own_way, lambda: across_copies(index), sent)
+    each(hands_over, hand_over, sent)
+    each(helps, help_across, sent)
 
     @pl.when(has_up)
     def _():
@@ -702,14 +767,13 @@
 
 
 def write_out(own, packed, sums, final_hbm, stored_hbm, stats_out, sem):
-    copies = [
-        pltpu.make_async_copy(packed.at[step], stored_hbm.at[0, step], sem.at[step]) for step in range(STEPS)
-    ]
-    copies.append(
-        pltpu.make_async_copy(
-            own.at[:, pl.ds(OWN, DEPTH), pl.ds(PAD, ROWS), :], final_hbm.at[0], sem.at[STEPS]
-        )
-    )
+    copies = []
+    for part in range(0, 9, 3):
+        parts = pl.ds(part, 3)
+        for step in range(STEPS):
+            copies.append((packed.at[step, parts], stored_hbm.at[0, step, parts]))
+        copies.append((own.at[parts, pl.ds(OWN, DEPTH), pl.ds(PAD, ROWS), :], final_hbm.at[0, parts]))
+    copies = [pltpu.make_async_copy(source, target, sem.at[k]) for k, (source, target) in enumerate(copies)]
     for copy in copies:
         copy.start()
     stats_out[...] = sums[...]
@@ -753,6 +817,7 @@
             pltpu.VMEM((2, max(LOW, slabs // LOW), 8, COLS), F32),
             pltpu.VMEM((STEPS, DEPTH, ROWS, COLS), F32),
             pltpu.VMEM((2 * DEPTH + 2 * MOD, ROWS, COLS), F32),
+            pltpu.VMEM((9, 6, ROWS - ROW_CUTS[1], COLS), BF16),
             dma((12,)),
             dma((STEPS, 2, 3)),
             dma((STEPS, 2, 3)),
@@ -760,6 +825,8 @@
             dma((2, 2)),
             dma((1 + 2 * parts,)),
             dma((1 + 2 * parts,)),
+            dma((2 + 2 * parts,)),
+            dma((2,)),
             dma((1 + parts, 2, 2)),
             dma((1 + parts, 2, 2)),
             dma((2, max(LOW, slabs // LOW))),
@@ -784,7 +851,7 @@
         ),
         in_specs=[vmem, vmem, vmem],
         out_specs=(hbm, hbm, vmem),
-        scratch_shapes=[dma((STEPS + 1,))],
+        scratch_shapes=[dma((12,))],
         compiler_params=pltpu.CompilerParams(vmem_limit_bytes=8 * 1024 * 1024),
         name="write_out",
     )(own, packed, statistics)

time: 60.8 us -> 57.2 us (0.941)
  Pallas kernels: 59.8 us -> 56 us
    pallas_call x1, Pallas kernels: 56.6 us -> 52.8 us  [per_device(): pl.pallas_call(functools.partial(kernel, slabs), out_shape=(pltpu.VMEM((9...]
where the time goes in v5:
time: 57.2 us; the launch traced here: 56.7 us
  Pallas kernels  56 us (98%)
  between operations  0.64 us (1%)
    pallas_call x1, Pallas kernels, per_device(): pl.pallas_call(functools.partial(kernel, slabs), out_shape=(pltpu.VMEM((9...  52.8 us
    pallas_call x1, Pallas kernels, per_device(): pl.pallas_call(write_out, out_shape=(jax.ShapeDtypeStruct(wavefield.shape...  3.21 us

profile of v5, /device:TPU:2, one launch (start us, length us, event | category | flops | bytes accessed | tf_op | source)
XLA Modules:
  0.0 56.7 jit_solution(3782287176556355263)
XLA Ops:
  0.6 52.8 %elastic_steps.1 = (f32[9,14,80,128]{3,2,1,0:T(8,128)S(1)}, bf16[3,9,8,64,128]{4,3,2,1,0:T(8,128)(2,1)S(1)}, f32[2,3]{1,0:T(2,128)S(1)}) custom-call(f32[1,9,8,64,128]{4,3,2,1,0:T(8,128)} %wave_hbm.1, f32[8,64,128]{2,1,0:T(8,128)} %buo_hbm.1, f32[8,64,128]{2,1,0:T(8,128)} %lame_hbm.1, f32[8,64,128]{2,1,0:T(8,128)} %shear_hbm.1, s32[72,16]{1,0:T(8,128)} %bitcast.5, ...), custom_call_target="tpu_custom_call" | custom-call | tf_op jit(solution)/shard_map/elastic_steps/pallas_call | solution.py:790
  53.5 3.2 %write_out.1 = (f32[1,9,8,64,128]{4,3,2,1,0:T(8,128)}, bf16[1,3,9,8,64,128]{5,4,3,2,1,0:T(8,128)(2,1)}, f32[2,3]{1,0:T(2,128)}) custom-call(f32[9,14,80,128]{3,2,1,0:T(8,128)S(1)} %get-tuple-element.9.own, bf16[3,9,8,64,128]{4,3,2,1,0:T(8,128)(2,1)S(1)} %get-tuple-element.10.packed, f32[2,3]{1,0:T(2,128)S(1)} %get-tuple-element.11.sums), custom_call_target="tpu_custom_call" | custom-call | tf_op jit(solution)/shard_map/write_out/pallas_call | solution.py:845

commit v6 on v5

--- a/solution.py
+++ b/solution.py
@@ -18,7 +18,7 @@
 PAD = 8
 YB = 16
 GROUP = 2
-WIDE_GROUP = 4
+WIDE_GROUP = 9
 MATMUL_X = False
 OWN = 3
 FAR = 6
@@ -725,7 +725,8 @@
 
     pass_on(2)
     pl.when(late_sums)(second_phase)
-    recompute(0, lambda: pass_on(3))
+    pl.when(hands_over)(lambda: pass_on(3))
+    recompute(0, lambda: pl.when(own_way)(lambda: pass_on(3)))
     pl.when(jnp.logical_not(late_sums))(second_phase)
     recompute(1, lambda: None)
 

time: 57.2 us -> 55 us (0.962)
  Pallas kernels: 56 us -> 54.2 us
    pallas_call x1, Pallas kernels: 52.8 us -> 51 us  [per_device(): pl.pallas_call(functools.partial(kernel, slabs), out_shape=(pltpu.VMEM((9...]
where the time goes in v6:
time: 55 us; the launch traced here: 54.8 us
  Pallas kernels  54.2 us (99%)
  between operations  0.64 us (1%)
    pallas_call x1, Pallas kernels, per_device(): pl.pallas_call(functools.partial(kernel, slabs), out_shape=(pltpu.VMEM((9...  51 us
    pallas_call x1, Pallas kernels, per_device(): pl.pallas_call(write_out, out_shape=(jax.ShapeDtypeStruct(wavefield.shape...  3.21 us

profile of v6, /device:TPU:2, one launch (start us, length us, event | category | flops | bytes accessed | tf_op | source)
XLA Modules:
  0.0 54.8 jit_solution(16981071353191318166)
XLA Ops:
  0.6 51.0 %elastic_steps.1 = (f32[9,14,80,128]{3,2,1,0:T(8,128)S(1)}, bf16[3,9,8,64,128]{4,3,2,1,0:T(8,128)(2,1)S(1)}, f32[2,3]{1,0:T(2,128)S(1)}) custom-call(f32[1,9,8,64,128]{4,3,2,1,0:T(8,128)} %wave_hbm.1, f32[8,64,128]{2,1,0:T(8,128)} %buo_hbm.1, f32[8,64,128]{2,1,0:T(8,128)} %lame_hbm.1, f32[8,64,128]{2,1,0:T(8,128)} %shear_hbm.1, s32[72,16]{1,0:T(8,128)} %bitcast.5, ...), custom_call_target="tpu_custom_call" | custom-call | tf_op jit(solution)/shard_map/elastic_steps/pallas_call | solution.py:791
  51.6 3.2 %write_out.1 = (f32[1,9,8,64,128]{4,3,2,1,0:T(8,128)}, bf16[1,3,9,8,64,128]{5,4,3,2,1,0:T(8,128)(2,1)}, f32[2,3]{1,0:T(2,128)}) custom-call(f32[9,14,80,128]{3,2,1,0:T(8,128)S(1)} %get-tuple-element.9.own, bf16[3,9,8,64,128]{4,3,2,1,0:T(8,128)(2,1)S(1)} %get-tuple-element.10.packed, f32[2,3]{1,0:T(2,128)S(1)} %get-tuple-element.11.sums), custom_call_target="tpu_custom_call" | custom-call | tf_op jit(solution)/shard_map/write_out/pallas_call | solution.py:846

commit v7 on v6

--- a/solution.py
+++ b/solution.py
@@ -423,6 +423,13 @@
 
     own_way = jnp.logical_not(hands_over)
 
+    at_face = below_cross | above_cross
+    helps_face = (me == half - 1 - LOW) | (me == half + LOW)
+    hand_both, help_both = hands_over & jnp.logical_not(at_face), helps & jnp.logical_not(helps_face)
+
+    def goes(index):
+        return own_way | at_face if index == 3 else own_way
+
     def across_copies(index):
         return [across(0)] if index == 0 else [across(2 * index - 1), across(2 * index)]
 
@@ -431,27 +438,32 @@
             for copy in across_copies(index):
                 copy.start()
         else:
-            each(own_way, lambda: across_copies(index), begin)
-        each(below_cross, lambda: straight_up(index), begin)
-        each(above_cross, lambda: straight_down(index), begin)
-
-    late = pl.ds(ROW_CUTS[1], ROWS - ROW_CUTS[1])
-
-    def hand_over():
+            each(goes(index), lambda: across_copies(index), begin)
+        if index == 0:
+            each(below_cross, lambda: straight_up(index), begin)
+            each(above_cross, lambda: straight_down(index), begin)
+
+    def hand_over(parts):
+        begin_row, count = ROW_CUTS[1], ROW_CUTS[1 + parts] - ROW_CUTS[1]
         return [
-            remote(mirror.at[1, :, pl.ds(first, 3), late], held_over.at[:, pl.ds(3 * k, 3)],
+            remote(mirror.at[1, :, pl.ds(first, 3), pl.ds(begin_row, count)],
+                   held_over.at[:, pl.ds(3 * k, 3), pl.ds(0, count)],
                    help_send.at[k], help_recv.at[k], (helper, peer))
             for k, first in enumerate((0, 5))
         ]
 
-    def help_across():
+    def help_across(parts):
         return [
             remote(held_over.at[:, pl.ds(3 * k, 3), pl.ds(lo - ROW_CUTS[1], hi - lo)],
                    got.at[:, pl.ds(FAR + first, 3), pl.ds(lo, hi - lo)],
                    help_send.at[2 * i + k], x_recv.at[2 * i - 1 + k], (helped, 1 - peer))
-            for i, (lo, hi) in enumerate(row_parts, 1) if i > 1
+            for i, (lo, hi) in enumerate(row_parts, 1) if 1 < i <= 1 + parts
             for k, first in enumerate((0, 5))
         ]
+
+    def help_out(flagged, parts_given):
+        each(flagged, lambda: hand_over(parts_given), lambda copy: copy.wait_recv())
+        each(flagged, lambda: help_across(parts_given), begin)
 
     def send_rest():
         for index in range(2, len(row_parts) + 1):
@@ -653,6 +665,8 @@
                 for z in range(3):
                     own[part + 6, OWN + DEPTH + z, inner, :] = high_b[step, part, z].astype(F32)
 
+        pl.when((step == 1) & hand_both)(lambda: send_across(1))
+
         @pl.when((step == 2) & held)
         def _():
             send_rest()
@@ -669,24 +683,23 @@
         @pl.when(step == 0)
         def _():
             send_mats(1)
-            each(hands_over, hand_over, begin)
+            each(hand_both, lambda: hand_over(2), begin)
+            each(at_face, lambda: hand_over(1), begin)
             pl.when(own_way)(lambda: send_across(1))
+            for index in (1, 2, 3):
+                each(below_cross, lambda: straight_up(index), begin)
+                each(above_cross, lambda: straight_down(index), begin)
 
         @pl.when((step == 1) & jnp.logical_not(held))
         def _():
-            pl.when(hands_over)(lambda: send_across(1))
+            pl.when(at_face)(lambda: send_across(1))
+            help_out(help_both, 2)
             send_rest()
 
+        pl.when((step == 2) & hands_over)(lambda: pass_on(1))
         tally(step)
 
-    pl.when(hands_over)(lambda: pass_on(1))
-
-    @pl.when(helps)
-    def _():
-        for copy in hand_over():
-            copy.wait_recv()
-        for copy in help_across():
-            copy.start()
+    help_out(helps_face, 1)
 
     row8 = lax.broadcasted_iota(jnp.int32, (8, COLS), 0)
     lane8 = lanes((8, COLS))
@@ -740,9 +753,11 @@
         for copy in across_copies(index):
             copy.wait_send()
     for index in range(2, len(row_parts) + 1):
-        each(own_way, lambda: across_copies(index), sent)
-    each(hands_over, hand_over, sent)
-    each(helps, help_across, sent)
+        each(goes(index), lambda: across_copies(index), sent)
+    each(hand_both, lambda: hand_over(2), sent)
+    each(at_face, lambda: hand_over(1), sent)
+    each(help_both, lambda: help_across(2), sent)
+    each(helps_face, lambda: help_across(1), sent)
 
     @pl.when(has_up)
     def _():

time: 55 us -> 56 us (1.018)
  Pallas kernels: 54.2 us -> 55.2 us
    pallas_call x1, Pallas kernels: 51 us -> 52 us  [per_device(): pl.pallas_call(functools.partial(kernel, slabs), out_shape=(pltpu.VMEM((9...]
where the time goes in v7:
time: 56 us; the launch traced here: 55.8 us
  Pallas kernels  55.2 us (99%)
  between operations  0.64 us (1%)
    pallas_call x1, Pallas kernels, per_device(): pl.pallas_call(functools.partial(kernel, slabs), out_shape=(pltpu.VMEM((9...  52 us
    pallas_call x1, Pallas kernels, per_device(): pl.pallas_call(write_out, out_shape=(jax.ShapeDtypeStruct(wavefield.shape...  3.21 us

profile of v7, /device:TPU:2, one launch (start us, length us, event | category | flops | bytes accessed | tf_op | source)
XLA Modules:
  0.0 55.8 jit_solution(16792713332120408281)
XLA Ops:
  0.6 52.0 %elastic_steps.1 = (f32[9,14,80,128]{3,2,1,0:T(8,128)S(1)}, bf16[3,9,8,64,128]{4,3,2,1,0:T(8,128)(2,1)S(1)}, f32[2,3]{1,0:T(2,128)S(1)}) custom-call(f32[1,9,8,64,128]{4,3,2,1,0:T(8,128)} %wave_hbm.1, f32[8,64,128]{2,1,0:T(8,128)} %buo_hbm.1, f32[8,64,128]{2,1,0:T(8,128)} %lame_hbm.1, f32[8,64,128]{2,1,0:T(8,128)} %shear_hbm.1, s32[72,16]{1,0:T(8,128)} %bitcast.5, ...), custom_call_target="tpu_custom_call" | custom-call | tf_op jit(solution)/shard_map/elastic_steps/pallas_call | solution.py:806
  52.6 3.2 %write_out.1 = (f32[1,9,8,64,128]{4,3,2,1,0:T(8,128)}, bf16[1,3,9,8,64,128]{5,4,3,2,1,0:T(8,128)(2,1)}, f32[2,3]{1,0:T(2,128)}) custom-call(f32[9,14,80,128]{3,2,1,0:T(8,128)S(1)} %get-tuple-element.9.own, bf16[3,9,8,64,128]{4,3,2,1,0:T(8,128)(2,1)S(1)} %get-tuple-element.10.packed, f32[2,3]{1,0:T(2,128)S(1)} %get-tuple-element.11.sums), custom_call_target="tpu_custom_call" | custom-call | tf_op jit(solution)/shard_map/write_out/pallas_call | solution.py:861
